TPU v7x, 8 devices: a whole 2x2x1 slice. The times are simulated.
8 devices in a mesh: dp: 2 (over z, y), cp: 4 (over x, core).
Axes of the slice: x: 2, y: 2, z: 1, core: 2. Of those that a mesh axis runs over, the one named last changes fastest.
Arguments:
- x_in: bfloat16 [512, 5120], P(('dp', 'cp')), parts along dimension 0
- cache_k1: bfloat16 [2048, 40, 128], P(('dp', 'cp')), parts along dimension 0
- cache_v1: bfloat16 [2048, 40, 128], P(('dp', 'cp')), parts along dimension 0
- w_q1: bfloat16 [5120, 5120], replicated
- b_q1: bfloat16 [5120], replicated
- w_k1: bfloat16 [5120, 5120], replicated
- b_k1: bfloat16 [5120], replicated
- w_v1: bfloat16 [5120, 5120], replicated
- w_o1: bfloat16 [5120, 5120], replicated
- w_gate: bfloat16 [5120, 13824], replicated
- w_up: bfloat16 [5120, 13824], replicated
- w_down: bfloat16 [13824, 5120], replicated
- cache_k2: bfloat16 [2048, 40, 128], P(('dp', 'cp')), parts along dimension 0
- cache_v2: bfloat16 [2048, 40, 128], P(('dp', 'cp')), parts along dimension 0
- w_q2: bfloat16 [5120, 5120], replicated
- b_q2: bfloat16 [5120], replicated
- w_k2: bfloat16 [5120, 5120], replicated
- b_k2: bfloat16 [5120], replicated
- w_v2: bfloat16 [5120, 5120], replicated
- w_o2: bfloat16 [5120, 5120], replicated
Outputs:
- output 1: bfloat16 [512, 5120], P(('dp', 'cp')), parts along dimension 0
- output 2: bfloat16 [512, 5120], P(('dp', 'cp')), parts along dimension 0
- output 3: bfloat16 [512, 40, 128], P(('dp', 'cp')), parts along dimension 0
- output 4: bfloat16 [512, 40, 128], P(('dp', 'cp')), parts along dimension 0
- output 5: bfloat16 [512, 40, 128], P(('dp', 'cp')), parts along dimension 0
- output 6: bfloat16 [512, 40, 128], P(('dp', 'cp')), parts along dimension 0
There are 2 independent parts. A program takes and returns all parts, laid end to end along the dimension named above; an argument that names none is the same for every part.
All inputs are finite; a program needn't handle non-finite values.
Results may differ from a plain program's by a relative error of at most 0.0145851.
Values are sent between devices in bfloat16 or wider.
A program may use at most 3.25 GiB of HBM per device.

v0:
```python
import jax
import jax.numpy as jnp
from jax import lax
from jax.sharding import PartitionSpec as P

ROPE_THETA = 500000.0
NORM_EPS = 1e-5


def rms_norm(vals):
    wide = vals.astype(jnp.float32)
    return (wide * lax.rsqrt(jnp.mean(wide * wide, axis=-1, keepdims=True) + NORM_EPS)).astype(jnp.bfloat16)


def rope_tables(positions, head_dim):
    half_dim = head_dim // 2
    inv_freq = 1.0 / (ROPE_THETA ** (jnp.arange(half_dim, dtype=jnp.float32) * (2.0 / head_dim)))
    angles = positions.astype(jnp.float32)[:, None] * inv_freq[None, :]
    return jnp.cos(angles)[:, None, :], jnp.sin(angles)[:, None, :]


def apply_rope(vals, cos_t, sin_t):
    half_dim = vals.shape[-1] // 2
    first = vals[..., :half_dim]
    second = vals[..., half_dim:]
    return jnp.concatenate([first * cos_t - second * sin_t, second * cos_t + first * sin_t], axis=-1)


def project_rows(layer_in, w_q, b_q, w_k, b_k, w_v, positions, head_dim):
    rows = layer_in.shape[0]
    cos_t, sin_t = rope_tables(positions, head_dim)
    q_pre = (jnp.dot(layer_in, w_q, preferred_element_type=jnp.float32) + b_q.astype(jnp.float32)).astype(jnp.bfloat16)
    k_pre = (jnp.dot(layer_in, w_k, preferred_element_type=jnp.float32) + b_k.astype(jnp.float32)).astype(jnp.bfloat16)
    v_new = jnp.dot(layer_in, w_v, preferred_element_type=jnp.float32).astype(jnp.bfloat16).reshape(rows, -1, head_dim)
    q_rot = apply_rope(q_pre.reshape(rows, -1, head_dim).astype(jnp.float32), cos_t, sin_t).astype(jnp.bfloat16)
    k_new = apply_rope(k_pre.reshape(rows, -1, head_dim).astype(jnp.float32), cos_t, sin_t).astype(jnp.bfloat16)
    return q_rot, k_new, v_new


def mlp_block(resid_h, w_gate, w_up, w_down):
    normed = rms_norm(resid_h)
    gate_act = jnp.dot(normed, w_gate, preferred_element_type=jnp.float32).astype(jnp.bfloat16)
    up_proj = jnp.dot(normed, w_up, preferred_element_type=jnp.float32).astype(jnp.bfloat16)
    mixed = (jax.nn.silu(gate_act.astype(jnp.float32)) * up_proj.astype(jnp.float32)).astype(jnp.bfloat16)
    return (resid_h.astype(jnp.float32) + jnp.dot(mixed, w_down, preferred_element_type=jnp.float32)).astype(jnp.bfloat16)


def partial_attend(q_grp, keys, values, scale, visible):
    scores = jnp.einsum('tkgd,skd->tkgs', q_grp, keys, preferred_element_type=jnp.float32) * scale
    if visible is not None:
        scores = jnp.where(visible, scores, -jnp.inf)
    peak = jnp.max(scores, axis=-1)
    prob_w = jnp.exp(scores - peak[..., None])
    total = jnp.sum(prob_w, axis=-1)
    summed = jnp.einsum('tkgs,skd->tkgd', prob_w.astype(jnp.bfloat16), values, preferred_element_type=jnp.float32)
    return summed / total[..., None], peak + jnp.log(total)


def merge_parts(out_a, lse_a, out_b, lse_b):
    lse_new = jnp.logaddexp(lse_a, lse_b)
    merged = out_a * jnp.exp(lse_a - lse_new)[..., None] + out_b * jnp.exp(lse_b - lse_new)[..., None]
    return merged, lse_new


def attention_layer(layer_in, cache_k, cache_v, w_q, b_q, w_k, b_k, w_v, w_o, axis_size):
    tok_dev = layer_in.shape[0]
    cache_dev, kv_heads, head_dim = cache_k.shape
    heads = w_q.shape[1] // head_dim
    my_idx = lax.axis_index('cp')
    positions = axis_size * cache_dev + my_idx * tok_dev + jnp.arange(tok_dev)
    q_rot, k_new, v_new = project_rows(layer_in, w_q, b_q, w_k, b_k, w_v, positions, head_dim)
    q_grp = q_rot.reshape(tok_dev, kv_heads, heads // kv_heads, head_dim)
    scale = head_dim ** -0.5
    all_k = lax.all_gather(k_new, 'cp', axis=0, tiled=True)
    all_v = lax.all_gather(v_new, 'cp', axis=0, tiled=True)
    q_pos = my_idx * tok_dev + jnp.arange(tok_dev)
    visible = (jnp.arange(axis_size * tok_dev)[None, :] <= q_pos[:, None])[:, None, None, :]
    out_acc, lse_acc = partial_attend(q_grp, all_k, all_v, scale, visible)
    out_loc, lse_loc = partial_attend(q_grp, cache_k, cache_v, scale, None)
    out_acc, lse_acc = merge_parts(out_acc, lse_acc, out_loc, lse_loc)
    shift = [(src_idx, (src_idx + 1) % axis_size) for src_idx in range(axis_size)]

    def cache_step(step, carry):
        blk_k, blk_v, out_run, lse_run = carry
        blk_k = lax.ppermute(blk_k, 'cp', shift)
        blk_v = lax.ppermute(blk_v, 'cp', shift)
        out_blk, lse_blk = partial_attend(q_grp, blk_k, blk_v, scale, None)
        out_run, lse_run = merge_parts(out_run, lse_run, out_blk, lse_blk)
        return blk_k, blk_v, out_run, lse_run

    carry_end = lax.fori_loop(0, axis_size - 1, cache_step, (cache_k, cache_v, out_acc, lse_acc))
    o_half = carry_end[2].astype(jnp.bfloat16).reshape(tok_dev, heads * head_dim)
    y_out = jnp.dot(o_half, w_o, preferred_element_type=jnp.float32).astype(jnp.bfloat16)
    return y_out, k_new, v_new


def solution(mesh):
    axis_size = mesh.shape['cp']
    rows_spec = P(('dp', 'cp'), None)
    cache_spec = P(('dp', 'cp'), None, None)
    mat_spec = P(None, None)
    vec_spec = P(None)
    layer_specs = (cache_spec, cache_spec, mat_spec, vec_spec, mat_spec, vec_spec, mat_spec, mat_spec)
    in_specs = (rows_spec,) + layer_specs + (mat_spec, mat_spec, mat_spec) + layer_specs
    out_specs = (rows_spec, rows_spec, cache_spec, cache_spec, cache_spec, cache_spec)

    def forward(x_in, cache_k1, cache_v1, w_q1, b_q1, w_k1, b_k1, w_v1, w_o1, w_gate, w_up, w_down, cache_k2, cache_v2, w_q2, b_q2, w_k2, b_k2, w_v2, w_o2):
        y_one, k_one, v_one = attention_layer(x_in, cache_k1, cache_v1, w_q1, b_q1, w_k1, b_k1, w_v1, w_o1, axis_size)
        resid_h = (x_in.astype(jnp.float32) + y_one.astype(jnp.float32)).astype(jnp.bfloat16)
        hidden = mlp_block(resid_h, w_gate, w_up, w_down)
        y_two, k_two, v_two = attention_layer(rms_norm(hidden), cache_k2, cache_v2, w_q2, b_q2, w_k2, b_k2, w_v2, w_o2, axis_size)
        return hidden, y_two, k_one, v_one, k_two, v_two

    return jax.shard_map(forward, mesh=mesh, in_specs=in_specs, out_specs=out_specs, check_vma=False)
```

profile of v0, /device:TPU:0, one launch (start us, length us, event | category | flops | bytes accessed | tf_op | source)
XLA Modules:
  0.0 820.6 jit_solution(17713267954110736079)
XLA Ops:
  7.9 20.8 %fusion.70 = f32[8,8,40,128]{3,1,2,0:T(8,128)S(1)} fusion(bf16[64,5120]{1,0:T(8,128)(2,1)} %param.24, bf16[5120,5120]{1,0:T(8,128)(2,1)} %param.29, f32[5120]{0:T(1024)S(1)} %convert_element_type.156), kind=kOutput, calls=%fused_computation.105 | convolution fusion | flops 3356426240 | bytes 54415360 | tf_op jit(solution)/shard_map/dot_general | solution.py:33
  29.9 21.9 %fusion.69 = f32[8,8,40,128]{3,1,2,0:T(8,128)} fusion(bf16[64,5120]{1,0:T(8,128)(2,1)S(1)} %copy-done, bf16[5120,5120]{1,0:T(8,128)(2,1)} %param.27, f32[5120]{0:T(1024)S(1)} %convert_element_type.161), kind=kOutput, calls=%fused_computation.104 | convolution fusion | flops 3356426240 | bytes 54415360 | tf_op jit(solution)/shard_map/dot_general | solution.py:32
  58.0 21.6 %convolution_convert_fusion.5 = bf16[64,5120]{1,0:T(8,128)(2,1)} fusion(bf16[64,5120]{1,0:T(8,128)(2,1)S(1)} %copy-done, bf16[5120,5120]{1,0:T(8,128)(2,1)} %param.31), kind=kOutput, calls=%fused_computation.73 | convolution fusion | flops 3355770880 | bytes 53739520 | tf_op jit(solution)/shard_map/dot_general | solution.py:34
  96.2 11.5 %all-gather.5.cloned.1.call-done = bf16[256,40,128]{2,0,1:T(8,128)(2,1)} async-done(((bf16[64,40,128]{2,0,1:T(8,128)(2,1)}), bf16[256,40,128]{2,0,1:T(8,128)(2,1)}) %all-gather.5.cloned.1.call-update) | async-done | bytes 2621456 | tf_op jit(solution)/shard_map/all_gather | solution.py:75
  111.1 4.0 multiply_add_fusion.3
  115.0 202.8 %while.32 = (s32[]{:T(128)}, bf16[256,40,128]{2,0,1:T(8,128)(2,1)}, bf16[256,40,128]{2,0,1:T(8,128)(2,1)}, f32[64,40,1,128]{3,0,1,2:T(8,128)}, f32[64,40,1]{0,1,...) while((s32[]{:T(128)}, bf16[256,40,128]{2,0,1:T(8,128)(2,1)}, ...), condition=%wide.region_7.8_spmd, body=%wide.region_4.7_spmd.sunk | while | flops 342123520 | bytes 58491092 | solution.py:91
  115.5 30.6 %collective-permute-done = bf16[256,40,128]{2,0,1:T(8,128)(2,1)S(1)} collective-permute-done((bf16[256,40,128]{2,0,1:T(8,128)(2,1)}, bf16[256,40,128]{2,0,1:T(8,128)(2,1)S(1)}, u32[]{:S(2)}, u32[]{:S(2)}) %collective-permute-start) | collective-permute-done | bytes 2621472 | tf_op jit(solution)/shard_map/while/body/eval_jaxpr/ppermute | solution.py:85
  149.7 24.4 %collective-permute-done.1 = bf16[256,40,128]{2,0,1:T(8,128)(2,1)} collective-permute-done((bf16[256,40,128]{2,0,1:T(8,128)(2,1)}, bf16[256,40,128]{2,0,1:T(8,128)(2,1)}, u32[]{:S(2)}, u32[]{:S(2)}) %collective-permute-start.1) | collective-permute-done | bytes 2621472 | tf_op jit(solution)/shard_map/while/body/eval_jaxpr/ppermute | solution.py:86
  177.8 3.7 multiply_add_fusion.6
  183.1 30.6 %collective-permute-done = bf16[256,40,128]{2,0,1:T(8,128)(2,1)S(1)} collective-permute-done((bf16[256,40,128]{2,0,1:T(8,128)(2,1)}, bf16[256,40,128]{2,0,1:T(8,128)(2,1)S(1)}, u32[]{:S(2)}, u32[]{:S(2)}) %collective-permute-start) | collective-permute-done | bytes 2621472 | tf_op jit(solution)/shard_map/while/body/eval_jaxpr/ppermute | solution.py:85
  217.3 24.4 %collective-permute-done.1 = bf16[256,40,128]{2,0,1:T(8,128)(2,1)} collective-permute-done((bf16[256,40,128]{2,0,1:T(8,128)(2,1)}, bf16[256,40,128]{2,0,1:T(8,128)(2,1)}, u32[]{:S(2)}, u32[]{:S(2)}) %collective-permute-start.1) | collective-permute-done | bytes 2621472 | tf_op jit(solution)/shard_map/while/body/eval_jaxpr/ppermute | solution.py:86
  245.4 3.7 multiply_add_fusion.6
  250.7 30.6 %collective-permute-done = bf16[256,40,128]{2,0,1:T(8,128)(2,1)S(1)} collective-permute-done((bf16[256,40,128]{2,0,1:T(8,128)(2,1)}, bf16[256,40,128]{2,0,1:T(8,128)(2,1)S(1)}, u32[]{:S(2)}, u32[]{:S(2)}) %collective-permute-start) | collective-permute-done | bytes 2621472 | tf_op jit(solution)/shard_map/while/body/eval_jaxpr/ppermute | solution.py:85
  285.0 24.4 %collective-permute-done.1 = bf16[256,40,128]{2,0,1:T(8,128)(2,1)} collective-permute-done((bf16[256,40,128]{2,0,1:T(8,128)(2,1)}, bf16[256,40,128]{2,0,1:T(8,128)(2,1)}, u32[]{:S(2)}, u32[]{:S(2)}) %collective-permute-start.1) | collective-permute-done | bytes 2621472 | tf_op jit(solution)/shard_map/while/body/eval_jaxpr/ppermute | solution.py:86
  313.0 3.7 multiply_add_fusion.6
  319.8 20.6 %multiply_reduce_fusion = (f32[64]{0:T(128)S(1)}, f32[64,5120]{1,0:T(8,128)S(1)}) fusion(bf16[5120,5120]{1,0:T(8,128)(2,1)} %param.32, bf16[8,8,40,128]{3,2,1,0:T(8,128)(2,1)S(1)} %bitcast.345, bf16[64,5120]{1,0:T(8,128)(2,1)S(1)} %copy-done.1), kind=kOutput, calls=%fused_computation.124 | convolution fusion | flops 3358064640 | bytes 55050496 | tf_op jit(solution)/shard_map/dot_general | solution.py:93
  340.4 47.7 %fusion.35 = f32[64,13824]{1,0:T(8,128)} fusion(bf16[5120,13824]{1,0:T(8,128)(2,1)} %param.33, f32[64,5120]{1,0:T(8,128)S(1)} %get-tuple-element.173, f32[64]{0:T(128)S(1)} %add_rsqrt_fusion.1), kind=kOutput, calls=%fused_computation.51 | convolution fusion | flops 9062121472 | bytes 146407680 | tf_op jit(solution)/shard_map/dot_general | solution.py:42
  388.1 49.0 %fusion.34.clone.1.clone.4 = bf16[64,13824]{1,0:T(8,128)(2,1)} fusion(bf16[5120,13824]{1,0:T(8,128)(2,1)} %param.34, f32[64,13824]{1,0:T(8,128)} %fusion.35, f32[64,5120]{1,0:T(8,128)S(1)} %get-tuple-element.173, f32[64]{0:T(128)S(1)} %add_rsqrt_fusion.1), kind=kOutput, calls=%fused_computation.49.clone.clone.clone.clone.clone.1 | convolution fusion | flops 9067429888 | bytes 148177152 | tf_op jit(solution)/shard_map/dot_general | solution.py:43
  437.1 47.3 %fusion.71 = (f32[64]{0:T(128)S(1)}, bf16[64,5120]{1,0:T(8,128)(2,1)S(1)}) fusion(f32[64,5120]{1,0:T(8,128)S(1)} %get-tuple-element.173, bf16[13824,5120]{1,0:T(8,128)(2,1)} %param.35, bf16[64,13824]{1,0:T(8,128)(2,1)} %fusion.34.clone.1.clone.4), kind=kOutput, calls=%fused_computation.110 | convolution fusion | flops 9061335040 | bytes 145293568 | tf_op jit(solution)/shard_map/dot_general | solution.py:45
  484.4 20.9 %fusion.68 = f32[8,8,40,128]{3,1,2,0:T(8,128)S(1)} fusion(bf16[5120,5120]{1,0:T(8,128)(2,1)} %param.40, f32[5120]{0:T(1024)S(1)} %copy-done.31, bf16[64,5120]{1,0:T(8,128)(2,1)S(1)} %get-tuple-element.175, f32[64]{0:T(128)S(1)} %add_rsqrt_fusion), kind=kOutput, calls=%fused_computation.103 | convolution fusion | flops 3357409280 | bytes 54415616 | tf_op jit(solution)/shard_map/dot_general | solution.py:33
  506.3 22.0 %fusion.67 = f32[8,8,40,128]{3,1,2,0:T(8,128)} fusion(bf16[5120,5120]{1,0:T(8,128)(2,1)} %param.38, f32[5120]{0:T(1024)S(1)} %copy-done.30, bf16[64,5120]{1,0:T(8,128)(2,1)S(1)} %get-tuple-element.175, f32[64]{0:T(128)S(1)} %add_rsqrt_fusion), kind=kOutput, calls=%fused_computation.102 | convolution fusion | flops 3357409280 | bytes 54415616 | tf_op jit(solution)/shard_map/dot_general | solution.py:32
  534.0 20.7 %convolution_convert_fusion.3 = bf16[64,5120]{1,0:T(8,128)(2,1)S(1)} fusion(bf16[5120,5120]{1,0:T(8,128)(2,1)} %param.42, bf16[64,5120]{1,0:T(8,128)(2,1)S(1)} %get-tuple-element.175, f32[64]{0:T(128)S(1)} %add_rsqrt_fusion), kind=kOutput, calls=%fused_computation.67 | convolution fusion | flops 3356753920 | bytes 53739776 | tf_op jit(solution)/shard_map/dot_general | solution.py:34
  574.2 6.1 all-gather.9.cloned.1.call-done
  587.2 203.1 %while.33 = (s32[]{:T(128)}, bf16[256,40,128]{2,0,1:T(8,128)(2,1)}, bf16[256,40,128]{2,0,1:T(8,128)(2,1)}, f32[64,40,1,128]{3,0,1,2:T(8,128)}, f32[64,40,1]{0,1,...) while((s32[]{:T(128)}, bf16[256,40,128]{2,0,1:T(8,128)(2,1)}, ...), condition=%wide.region_17.18_spmd, body=%wide.region_14.17_spmd.sunk | while | flops 342123520 | bytes 58491092 | solution.py:91
  587.9 30.6 %collective-permute-done.2 = bf16[256,40,128]{2,0,1:T(8,128)(2,1)S(1)} collective-permute-done((bf16[256,40,128]{2,0,1:T(8,128)(2,1)}, bf16[256,40,128]{2,0,1:T(8,128)(2,1)S(1)}, u32[]{:S(2)}, u32[]{:S(2)}) %collective-permute-start.2) | collective-permute-done | bytes 2621472 | tf_op jit(solution)/shard_map/while/body/eval_jaxpr/ppermute | solution.py:85
  622.2 24.4 %collective-permute-done.3 = bf16[256,40,128]{2,0,1:T(8,128)(2,1)} collective-permute-done((bf16[256,40,128]{2,0,1:T(8,128)(2,1)}, bf16[256,40,128]{2,0,1:T(8,128)(2,1)}, u32[]{:S(2)}, u32[]{:S(2)}) %collective-permute-start.3) | collective-permute-done | bytes 2621472 | tf_op jit(solution)/shard_map/while/body/eval_jaxpr/ppermute | solution.py:86
  655.5 30.6 %collective-permute-done.2 = bf16[256,40,128]{2,0,1:T(8,128)(2,1)S(1)} collective-permute-done((bf16[256,40,128]{2,0,1:T(8,128)(2,1)}, bf16[256,40,128]{2,0,1:T(8,128)(2,1)S(1)}, u32[]{:S(2)}, u32[]{:S(2)}) %collective-permute-start.2) | collective-permute-done | bytes 2621472 | tf_op jit(solution)/shard_map/while/body/eval_jaxpr/ppermute | solution.py:85
  689.8 24.4 %collective-permute-done.3 = bf16[256,40,128]{2,0,1:T(8,128)(2,1)} collective-permute-done((bf16[256,40,128]{2,0,1:T(8,128)(2,1)}, bf16[256,40,128]{2,0,1:T(8,128)(2,1)}, u32[]{:S(2)}, u32[]{:S(2)}) %collective-permute-start.3) | collective-permute-done | bytes 2621472 | tf_op jit(solution)/shard_map/while/body/eval_jaxpr/ppermute | solution.py:86
  723.1 30.6 %collective-permute-done.2 = bf16[256,40,128]{2,0,1:T(8,128)(2,1)S(1)} collective-permute-done((bf16[256,40,128]{2,0,1:T(8,128)(2,1)}, bf16[256,40,128]{2,0,1:T(8,128)(2,1)S(1)}, u32[]{:S(2)}, u32[]{:S(2)}) %collective-permute-start.2) | collective-permute-done | bytes 2621472 | tf_op jit(solution)/shard_map/while/body/eval_jaxpr/ppermute | solution.py:85
  757.4 24.4 %collective-permute-done.3 = bf16[256,40,128]{2,0,1:T(8,128)(2,1)} collective-permute-done((bf16[256,40,128]{2,0,1:T(8,128)(2,1)}, bf16[256,40,128]{2,0,1:T(8,128)(2,1)}, u32[]{:S(2)}, u32[]{:S(2)}) %collective-permute-start.3) | collective-permute-done | bytes 2621472 | tf_op jit(solution)/shard_map/while/body/eval_jaxpr/ppermute | solution.py:86
  785.4 3.7 multiply_add_fusion.7
  792.1 21.5 %convolution_convert_fusion.2 = bf16[64,5120]{1,0:T(8,128)(2,1)} fusion(bf16[5120,5120]{1,0:T(8,128)(2,1)} %param.43, bf16[8,8,40,128]{3,2,1,0:T(8,128)(2,1)S(1)} %bitcast.344), kind=kOutput, calls=%fused_computation.66 | convolution fusion | flops 3355770880 | bytes 53739520 | tf_op jit(solution)/shard_map/dot_general | solution.py:93
  (197 shorter events, 124.8 us)
Async XLA Ops:
  7.2 84.6 %all-gather.7.cloned.1.call-start = ((), (), s32[]{:S(2)}) async-start(), calls=%async_computation.1 | async-start | bytes 3276800 | tf_op jit(solution)/shard_map/all_gather | solution.py:74
  57.8 50.0 %all-gather.5.cloned.1.call-start = ((), (), s32[]{:S(2)}) async-start(), calls=%async_computation | async-start | bytes 3276800 | tf_op jit(solution)/shard_map/all_gather | solution.py:75
  58.0 23.8 %copy-start.3 = (bf16[256,40,128]{2,1,0:T(8,128)(2,1)S(1)}, bf16[256,40,128]{2,1,0:T(8,128)(2,1)}, u32[]{:S(2)}) copy-start(bf16[256,40,128]{2,1,0:T(8,128)(2,1)} %param.25) | copy-start | bytes 7864324
  81.8 487.9 %all-gather.11.cloned.1.call-start = ((), (), s32[]{:S(2)}) async-start(), calls=%async_computation.3 | async-start | bytes 3276800 | tf_op jit(solution)/shard_map/all_gather | solution.py:74
  84.0 3.4 copy-start.10
  84.0 3.4 copy-start.11
  84.0 3.9 copy-start.4
  87.9 19.8 %copy-start.24 = (pred[64,256]{1,0:T(8,128)(4,1)}, pred[64,256]{1,0:T(8,128)(4,1)S(1)}, u32[]{:S(2)}) copy-start(pred[64,256]{1,0:T(8,128)(4,1)S(1)} %iota_compare_fusion) | copy-start | bytes 49156
  107.7 3.3 copy-start.17
  115.0 31.1 %collective-permute-start = (bf16[256,40,128]{2,0,1:T(8,128)(2,1)}, bf16[256,40,128]{2,0,1:T(8,128)(2,1)S(1)}, u32[]{:S(2)}, u32[]{:S(2)}) collective-permute-start(bf16[256,40,128]{2,0,1:T(8,128)(2,1)} %get-tuple-element.280), channel_id=1, source_target_pairs={{0,1},{1,2},{2,3},{3,0},{4,5},{5,6},{6,7},{7,4}} | collective-permute-start | bytes 7864328 | tf_op jit(solution)/shard_map/while/body/eval_jaxpr/ppermute | solution.py:85
  115.2 58.9 %collective-permute-start.1 = (bf16[256,40,128]{2,0,1:T(8,128)(2,1)}, bf16[256,40,128]{2,0,1:T(8,128)(2,1)}, u32[]{:S(2)}, u32[]{:S(2)}) collective-permute-start(bf16[256,40,128]{2,0,1:T(8,128)(2,1)} %get-tuple-element.281), channel_id=1, source_target_pairs={{0,1},{1,2},{2,3},{3,0},{4,5},{5,6},{6,7},{7,4}} | collective-permute-start | bytes 7864328 | tf_op jit(solution)/shard_map/while/body/eval_jaxpr/ppermute | solution.py:86
  149.7 28.0 %copy-start.20 = (f32[64,40,1,128]{3,0,1,2:T(8,128)S(1)}, f32[64,40,1,128]{3,0,1,2:T(8,128)}, u32[]{:S(2)}) copy-start(f32[64,40,1,128]{3,0,1,2:T(8,128)} %get-tuple-element.282) | copy-start | bytes 3932164 | tf_op jit(solution)/shard_map/while
  182.6 31.1 %collective-permute-start = (bf16[256,40,128]{2,0,1:T(8,128)(2,1)}, bf16[256,40,128]{2,0,1:T(8,128)(2,1)S(1)}, u32[]{:S(2)}, u32[]{:S(2)}) collective-permute-start(bf16[256,40,128]{2,0,1:T(8,128)(2,1)} %get-tuple-element.280), channel_id=1, source_target_pairs={{0,1},{1,2},{2,3},{3,0},{4,5},{5,6},{6,7},{7,4}} | collective-permute-start | bytes 7864328 | tf_op jit(solution)/shard_map/while/body/eval_jaxpr/ppermute | solution.py:85
  182.6 59.2 %collective-permute-start.1 = (bf16[256,40,128]{2,0,1:T(8,128)(2,1)}, bf16[256,40,128]{2,0,1:T(8,128)(2,1)}, u32[]{:S(2)}, u32[]{:S(2)}) collective-permute-start(bf16[256,40,128]{2,0,1:T(8,128)(2,1)} %get-tuple-element.281), channel_id=1, source_target_pairs={{0,1},{1,2},{2,3},{3,0},{4,5},{5,6},{6,7},{7,4}} | collective-permute-start | bytes 7864328 | tf_op jit(solution)/shard_map/while/body/eval_jaxpr/ppermute | solution.py:86
  217.3 28.0 %copy-start.20 = (f32[64,40,1,128]{3,0,1,2:T(8,128)S(1)}, f32[64,40,1,128]{3,0,1,2:T(8,128)}, u32[]{:S(2)}) copy-start(f32[64,40,1,128]{3,0,1,2:T(8,128)} %get-tuple-element.282) | copy-start | bytes 3932164 | tf_op jit(solution)/shard_map/while
  250.2 31.1 %collective-permute-start = (bf16[256,40,128]{2,0,1:T(8,128)(2,1)}, bf16[256,40,128]{2,0,1:T(8,128)(2,1)S(1)}, u32[]{:S(2)}, u32[]{:S(2)}) collective-permute-start(bf16[256,40,128]{2,0,1:T(8,128)(2,1)} %get-tuple-element.280), channel_id=1, source_target_pairs={{0,1},{1,2},{2,3},{3,0},{4,5},{5,6},{6,7},{7,4}} | collective-permute-start | bytes 7864328 | tf_op jit(solution)/shard_map/while/body/eval_jaxpr/ppermute | solution.py:85
  250.2 59.2 %collective-permute-start.1 = (bf16[256,40,128]{2,0,1:T(8,128)(2,1)}, bf16[256,40,128]{2,0,1:T(8,128)(2,1)}, u32[]{:S(2)}, u32[]{:S(2)}) collective-permute-start(bf16[256,40,128]{2,0,1:T(8,128)(2,1)} %get-tuple-element.281), channel_id=1, source_target_pairs={{0,1},{1,2},{2,3},{3,0},{4,5},{5,6},{6,7},{7,4}} | collective-permute-start | bytes 7864328 | tf_op jit(solution)/shard_map/while/body/eval_jaxpr/ppermute | solution.py:86
  284.9 28.0 %copy-start.20 = (f32[64,40,1,128]{3,0,1,2:T(8,128)S(1)}, f32[64,40,1,128]{3,0,1,2:T(8,128)}, u32[]{:S(2)}) copy-start(f32[64,40,1,128]{3,0,1,2:T(8,128)} %get-tuple-element.282) | copy-start | bytes 3932164 | tf_op jit(solution)/shard_map/while
  437.1 47.3 %copy-start.31 = (f32[5120]{0:T(1024)S(1)}, f32[5120]{0:T(1024)}, u32[]{:S(2)}) copy-start(f32[5120]{0:T(1024)} %convert_element_type.182) | copy-start | bytes 61444
  484.3 49.6 %copy-start.2 = (bf16[64,5120]{1,0:T(8,128)(2,1)}, bf16[64,5120]{1,0:T(8,128)(2,1)S(1)}, u32[]{:S(2)}) copy-start(bf16[64,5120]{1,0:T(8,128)(2,1)S(1)} %get-tuple-element.175) | copy-start | bytes 1966084
  533.9 46.4 %all-gather.9.cloned.1.call-start = ((), (), s32[]{:S(2)}) async-start(), calls=%async_computation.2 | async-start | bytes 3276800 | tf_op jit(solution)/shard_map/all_gather | solution.py:75
  554.6 3.4 copy-start.5
  580.3 3.3 copy-start.19
  587.4 31.1 %collective-permute-start.2 = (bf16[256,40,128]{2,0,1:T(8,128)(2,1)}, bf16[256,40,128]{2,0,1:T(8,128)(2,1)S(1)}, u32[]{:S(2)}, u32[]{:S(2)}) collective-permute-start(bf16[256,40,128]{2,0,1:T(8,128)(2,1)} %get-tuple-element.301), channel_id=1, source_target_pairs={{0,1},{1,2},{2,3},{3,0},{4,5},{5,6},{6,7},{7,4}} | collective-permute-start | bytes 7864328 | tf_op jit(solution)/shard_map/while/body/eval_jaxpr/ppermute | solution.py:85
  587.7 58.9 %collective-permute-start.3 = (bf16[256,40,128]{2,0,1:T(8,128)(2,1)}, bf16[256,40,128]{2,0,1:T(8,128)(2,1)}, u32[]{:S(2)}, u32[]{:S(2)}) collective-permute-start(bf16[256,40,128]{2,0,1:T(8,128)(2,1)} %get-tuple-element.302), channel_id=1, source_target_pairs={{0,1},{1,2},{2,3},{3,0},{4,5},{5,6},{6,7},{7,4}} | collective-permute-start | bytes 7864328 | tf_op jit(solution)/shard_map/while/body/eval_jaxpr/ppermute | solution.py:86
  622.2 28.0 %copy-start.22 = (f32[64,40,1,128]{3,0,1,2:T(8,128)S(1)}, f32[64,40,1,128]{3,0,1,2:T(8,128)}, u32[]{:S(2)}) copy-start(f32[64,40,1,128]{3,0,1,2:T(8,128)} %get-tuple-element.303) | copy-start | bytes 3932164 | tf_op jit(solution)/shard_map/while
  655.1 31.1 %collective-permute-start.2 = (bf16[256,40,128]{2,0,1:T(8,128)(2,1)}, bf16[256,40,128]{2,0,1:T(8,128)(2,1)S(1)}, u32[]{:S(2)}, u32[]{:S(2)}) collective-permute-start(bf16[256,40,128]{2,0,1:T(8,128)(2,1)} %get-tuple-element.301), channel_id=1, source_target_pairs={{0,1},{1,2},{2,3},{3,0},{4,5},{5,6},{6,7},{7,4}} | collective-permute-start | bytes 7864328 | tf_op jit(solution)/shard_map/while/body/eval_jaxpr/ppermute | solution.py:85
  655.1 59.2 %collective-permute-start.3 = (bf16[256,40,128]{2,0,1:T(8,128)(2,1)}, bf16[256,40,128]{2,0,1:T(8,128)(2,1)}, u32[]{:S(2)}, u32[]{:S(2)}) collective-permute-start(bf16[256,40,128]{2,0,1:T(8,128)(2,1)} %get-tuple-element.302), channel_id=1, source_target_pairs={{0,1},{1,2},{2,3},{3,0},{4,5},{5,6},{6,7},{7,4}} | collective-permute-start | bytes 7864328 | tf_op jit(solution)/shard_map/while/body/eval_jaxpr/ppermute | solution.py:86
  689.8 28.0 %copy-start.22 = (f32[64,40,1,128]{3,0,1,2:T(8,128)S(1)}, f32[64,40,1,128]{3,0,1,2:T(8,128)}, u32[]{:S(2)}) copy-start(f32[64,40,1,128]{3,0,1,2:T(8,128)} %get-tuple-element.303) | copy-start | bytes 3932164 | tf_op jit(solution)/shard_map/while
  722.7 31.1 %collective-permute-start.2 = (bf16[256,40,128]{2,0,1:T(8,128)(2,1)}, bf16[256,40,128]{2,0,1:T(8,128)(2,1)S(1)}, u32[]{:S(2)}, u32[]{:S(2)}) collective-permute-start(bf16[256,40,128]{2,0,1:T(8,128)(2,1)} %get-tuple-element.301), channel_id=1, source_target_pairs={{0,1},{1,2},{2,3},{3,0},{4,5},{5,6},{6,7},{7,4}} | collective-permute-start | bytes 7864328 | tf_op jit(solution)/shard_map/while/body/eval_jaxpr/ppermute | solution.py:85
  722.7 59.2 %collective-permute-start.3 = (bf16[256,40,128]{2,0,1:T(8,128)(2,1)}, bf16[256,40,128]{2,0,1:T(8,128)(2,1)}, u32[]{:S(2)}, u32[]{:S(2)}) collective-permute-start(bf16[256,40,128]{2,0,1:T(8,128)(2,1)} %get-tuple-element.302), channel_id=1, source_target_pairs={{0,1},{1,2},{2,3},{3,0},{4,5},{5,6},{6,7},{7,4}} | collective-permute-start | bytes 7864328 | tf_op jit(solution)/shard_map/while/body/eval_jaxpr/ppermute | solution.py:86
  757.4 28.0 %copy-start.22 = (f32[64,40,1,128]{3,0,1,2:T(8,128)S(1)}, f32[64,40,1,128]{3,0,1,2:T(8,128)}, u32[]{:S(2)}) copy-start(f32[64,40,1,128]{3,0,1,2:T(8,128)} %get-tuple-element.303) | copy-start | bytes 3932164 | tf_op jit(solution)/shard_map/while
  (27 other events, 49.2 us)
Sparse Core Ops, SparseCore 0:
  57.9 25.2 all-gather.6
  85.3 22.4 all-gather.4
  534.0 22.4 all-gather.10
  557.9 22.4 all-gather.8
where the time goes:
time: 829 us; the launch traced here: 821 us
  matrix products  364 us (44%)
  waiting for transfers between devices  348 us (42%)
  local copies, waits for them, and re-layouts  67.2 us (8%)
  other arithmetic  22.5 us (3%)
  between operations  14.7 us (2%)
    ppermute x6, waiting for transfers between devices, cache_step(): blk_k = lax.ppermute(blk_k, 'cp', shift)  184 us
    ppermute x6, waiting for transfers between devices, cache_step(): blk_v = lax.ppermute(blk_v, 'cp', shift)  147 us
    dot_general x1, matrix products, mlp_block(): jnp.dot(normed, w_up, preferred_element_type=jnp.float32)  49 us
    dot_general x1, matrix products, mlp_block(): jnp.dot(normed, w_gate, preferred_element_type=jnp.float32)  47.7 us
    dot_general x1, matrix products, mlp_block(): jnp.dot(mixed, w_down, preferred_element_type=jnp.float32)  47.3 us
    dot_general x2, matrix products, project_rows(): jnp.dot(layer_in, w_q, preferred_element_type=jnp.float32)  43.9 us
    dot_general x2, matrix products, project_rows(): jnp.dot(layer_in, w_v, preferred_element_type=jnp.float32)  42.3 us
    dot_general x2, matrix products, attention_layer(): jnp.dot(o_half, w_o, preferred_element_type=jnp.float32)  42.1 us
  transfers between devices with their start and end apart: 16, of which 14 were waited for; matrix products, arithmetic and copies ran while one was open for 12% of the time, Pallas kernels for 0%

commit v1 on v0

v1 whole, which is shorter than its diff:
```python
import functools

import jax
import jax.numpy as jnp
from jax import lax
from jax.experimental import pallas as pl
from jax.experimental.pallas import tpu as pltpu
from jax.sharding import PartitionSpec as P

ROPE_THETA = 500000.0
NORM_EPS = 1e-5
MESH = pl.DeviceIdType.MESH
F32 = jnp.float32
BF16 = jnp.bfloat16

TILE = 512
HEAD = 128
PER_BLOCK = TILE // HEAD
SLOTS = 7


def rope_tables(positions, head_dim):
    half_dim = head_dim // 2
    inv_freq = 1.0 / (ROPE_THETA ** (jnp.arange(half_dim, dtype=F32) * (2.0 / head_dim)))
    angles = positions.astype(F32)[:, None] * inv_freq[None, :]
    cos_t, sin_t = jnp.cos(angles), jnp.sin(angles)
    return jnp.concatenate([cos_t, cos_t], axis=1), jnp.concatenate([-sin_t, sin_t], axis=1)


def body(dims, cos_ref, sin_ref, bias_ref, x_hbm, ck1, cv1, ck2, cv2, wq1, wk1, wv1, wo1, w_gate, w_up, w_down,
         wq2, wk2, wv2, wo2, g_out, y_out, k1_out, v1_out, k2_out, v2_out,
         wring, xin, hbuf, nbuf, gbuf, ebuf, qcat, knew, vnew, kc, vc, o_loc, o_send, o_recv, obuf, ybuf,
         st_loc, st_send, st_recv,
         wsem, xsem, csem, qsend, qrecv, osend, orecv, ssend, srecv, dsend, drecv, asem, gsem):
    d_model, ff, rows, cache_rows = dims
    half = d_model // 2
    ffh = ff // 2
    ffc = ff // 3
    blocks = half // TILE
    ffn = ffh // (TILE // 2)
    crows = 2 * rows
    me = lax.axis_index("cp")
    core = lax.rem(me, 2)
    chip = me // 2
    partner = me + 1 - 2 * core
    peer = lax.rem(me + 2, 4)
    my_cols = pl.multiple_of(core * half, 128)
    my_rows = pl.multiple_of(core * rows, 16)
    other_rows = pl.multiple_of((1 - core) * rows, 16)
    other_cols = pl.multiple_of((1 - core) * half, 128)

    def col(b):
        return pl.multiple_of(core * half + b * TILE, 128)

    attn_tiles = 4 * blocks
    base1 = 0
    base_up = attn_tiles
    base_down = base_up + ffn
    base2 = base_down + 3 * blocks
    total = base2 + attn_tiles

    def start_full(w, b, slot):
        pltpu.make_async_copy(w.at[:, pl.ds(col(b), TILE)], wring.at[slot], wsem.at[slot]).start()

    def start_mlp(n, slot):
        at = pl.ds(pl.multiple_of(core * ffh + n * (TILE // 2), 128), TILE // 2)
        pltpu.make_async_copy(w_gate.at[:, at], wring.at[slot, :, pl.ds(0, TILE // 2)], wsem.at[slot]).start()
        pltpu.make_async_copy(w_up.at[:, at], wring.at[slot, :, pl.ds(TILE // 2, TILE // 2)], wsem.at[slot]).start()

    def start_down(i, slot):
        pltpu.make_async_copy(
            w_down.at[pl.ds(pl.multiple_of(lax.rem(i, 3) * ffc, 16), ffc), pl.ds(col(i // 3), TILE)],
            wring.at[slot, pl.ds(0, ffc), :], wsem.at[slot]).start()

    loop_end = 3 * (blocks - 1) + 1

    def attn_segments(base, wq, wk, wv, wo):
        return [
            (base, base + 1, lambda r, slot: start_full(wq, 0, slot), None),
            (base + 1, base + loop_end, lambda r, slot: start_full(wq, r // 3 + 1, slot), 0),
            (base + 1, base + loop_end, lambda r, slot: start_full(wk, r // 3, slot), 1),
            (base + 1, base + loop_end, lambda r, slot: start_full(wv, r // 3, slot), 2),
            (base + loop_end, base + loop_end + 1, lambda r, slot: start_full(wk, blocks - 1, slot), None),
            (base + loop_end + 1, base + loop_end + 2, lambda r, slot: start_full(wv, blocks - 1, slot), None),
            (base + loop_end + 2, base + attn_tiles, lambda r, slot: start_full(wo, r, slot), None),
        ]

    segments = attn_segments(base1, wq1, wk1, wv1, wo1) + [
        (base_up, base_down, start_mlp, None),
        (base_down, base2, start_down, None),
    ] + attn_segments(base2, wq2, wk2, wv2, wo2)

    def start_tile(s, lo, hi):
        slot = lax.rem(s, SLOTS) if not isinstance(s, int) else s % SLOTS
        for a, b, fn, phase in segments:
            if b <= lo or a >= hi:
                continue
            if isinstance(s, int):
                if a <= s < b and (phase is None or (s - a) % 3 == phase):
                    fn(s - a, slot)
                continue
            cond = (s >= a) & (s < b)
            if phase is not None:
                cond = cond & (lax.rem(s - a + 3, 3) == phase)

            @pl.when(cond)
            def _(a=a, fn=fn):
                fn(s - a, slot)

    def wait_tile(s, depth=None):
        slot = lax.rem(s, SLOTS) if not isinstance(s, int) else s % SLOTS
        ref = wring.at[slot] if depth is None else wring.at[slot, pl.ds(0, depth), :]
        pltpu.make_async_copy(ref, ref, wsem.at[slot]).wait()
        return slot

    def remote(src, dst, send, recv, who):
        return pltpu.make_async_remote_copy(src_ref=src, dst_ref=dst, send_sem=send, recv_sem=recv,
                                            device_id={"cp": who}, device_id_type=MESH)

    for s in range(SLOTS):
        start_tile(s, s, s + 1)

    barrier = pltpu.get_barrier_semaphore()
    for who in (partner, peer):
        pl.semaphore_signal(barrier, inc=1, device_id={"cp": who}, device_id_type=MESH)
    pl.semaphore_wait(barrier, 2)

    x_loc = pltpu.make_async_copy(x_hbm, xin.at[pl.ds(my_rows, rows)], xsem.at[0])
    x_rem = remote(x_hbm, xin.at[pl.ds(my_rows, rows)], xsem.at[1], xsem.at[2], partner)
    x_rem.start()
    x_loc.start()

    def cache_copies(ck, cv):
        crow = pl.ds(pl.multiple_of(core * cache_rows, 16), cache_rows)
        out = []
        for i, (src, dst) in enumerate(((ck, kc), (cv, vc))):
            out.append(pltpu.make_async_copy(src.at[:, pl.ds(my_cols, half)], dst.at[crow], csem.at[3 * i]))
            out.append(remote(src.at[:, pl.ds(other_cols, half)], dst.at[crow], csem.at[3 * i + 1], csem.at[3 * i + 2],
                              partner))
        return out

    cache1 = cache_copies(ck1, cv1)
    for c in cache1:
        c.start()
    x_loc.wait()
    x_rem.wait()

    def rope(vals):
        parts = []
        for i in range(PER_BLOCK):
            seg = vals[:, i * HEAD:(i + 1) * HEAD]
            parts.append(seg * cos_ref[...] + pltpu.roll(seg, HEAD // 2, 1) * sin_ref[...])
        return jnp.concatenate(parts, axis=1)

    def norm(src):
        step = 16

        @pl.loop(0, crows // step)
        def _(i):
            at = pl.ds(pl.multiple_of(i * step, step), step)
            wide = src[at, :].astype(F32)
            nbuf[at, :] = (wide * lax.rsqrt(jnp.mean(wide * wide, axis=-1, keepdims=True) + NORM_EPS)).astype(BF16)

    row_i = lax.broadcasted_iota(jnp.int32, (2 * crows, crows), 0)
    col_i = lax.broadcasted_iota(jnp.int32, (2 * crows, crows), 1)
    far_lim = jnp.where(chip == 0, crows, -1)
    scale = HEAD ** -0.5

    def attend(b):
        lane = lax.broadcasted_iota(jnp.int32, (2 * crows, HEAD), 1)
        visible = col_i <= jnp.where(row_i < crows, row_i, far_lim)
        stats = jnp.zeros((2 * crows, HEAD), F32)
        dims_t = (((1,), (1,)), ((), ()))
        for i in range(PER_BLOCK):
            at = pl.ds(i * HEAD, HEAD)
            cat = pl.ds(pl.multiple_of(b * TILE + i * HEAD, 128), HEAD)
            q = qcat[b, :, at]
            s_old = lax.dot_general(q, kc[:, cat], dims_t, preferred_element_type=F32) * scale
            s_new = lax.dot_general(q, knew[b, :, at], dims_t, preferred_element_type=F32) * scale
            s_new = jnp.where(visible, s_new, -jnp.inf)
            peak = jnp.maximum(jnp.max(s_old, axis=1, keepdims=True), jnp.max(s_new, axis=1, keepdims=True))
            p_old = jnp.exp(s_old - peak)
            p_new = jnp.exp(s_new - peak)
            total_p = jnp.sum(p_old, axis=1, keepdims=True) + jnp.sum(p_new, axis=1, keepdims=True)
            acc = jnp.dot(p_old.astype(BF16), vc[:, cat], preferred_element_type=F32)
            acc = acc + jnp.dot(p_new.astype(BF16), vnew[b, :, at], preferred_element_type=F32)
            o_loc[b, :, at] = acc[:crows]
            o_send[b, :, at] = acc[crows:]
            stats = jnp.where(lane == 2 * i, peak, stats)
            stats = jnp.where(lane == 2 * i + 1, total_p, stats)
        st_loc[b] = stats[:crows]
        st_send[b] = stats[crows:].T[:8, :]

    def q_copy(b):
        return remote(qcat.at[b, pl.ds(0, crows), :], qcat.at[b, pl.ds(crows, crows), :], qsend.at[b], qrecv.at[b], peer)

    def o_copy(b):
        return remote(o_send.at[b], o_recv.at[b], osend.at[b], orecv.at[b], peer)

    def s_copy(b):
        return remote(st_send.at[b], st_recv.at[b], ssend.at[b], srecv.at[b], peer)

    def attention(layer_in, base, bias_row, caches, k_out, v_out):
        def q_step(b, s, lo, hi):
            slot = wait_tile(s)
            pre = (jnp.dot(layer_in[...], wring[slot], preferred_element_type=F32)
                   + bias_ref[pl.ds(bias_row, 1), pl.ds(col(b), TILE)]).astype(BF16)
            start_tile(s + SLOTS, lo + SLOTS, hi + SLOTS)
            qcat[b, pl.ds(0, crows), :] = rope(pre.astype(F32)).astype(BF16)
            q_copy(b).start()

        q_step(0, base, base, base + 1)

        @pl.loop(0, blocks)
        def _(b):
            has_q = (2 * blocks - 3 - b) // (blocks - 1)
            s = base + 1 + 3 * b

            @pl.when(b < blocks - 1)
            def _():
                q_step(b + 1, s, base + 1, base + loop_end)

            s = s + has_q
            slot = wait_tile(s)
            pre = (jnp.dot(layer_in[...], wring[slot], preferred_element_type=F32)
                   + bias_ref[pl.ds(bias_row + 1, 1), pl.ds(col(b), TILE)]).astype(BF16)
            start_tile(s + SLOTS, base + 2 + SLOTS, base + loop_end + 2 + SLOTS)
            knew[b] = rope(pre.astype(F32)).astype(BF16)
            s = s + 1
            slot = wait_tile(s)
            vals = jnp.dot(layer_in[...], wring[slot], preferred_element_type=F32).astype(BF16)
            start_tile(s + SLOTS, base + 3 + SLOTS, base + loop_end + 2 + SLOTS)
            vnew[b] = vals

            @pl.when(b == 0)
            def _():
                for c in caches:
                    c.wait()

            q_copy(b).wait_recv()
            attend(b)
            for src, dst, k in ((knew, k_out, 0), (vnew, v_out, 3)):
                pltpu.make_async_copy(src.at[b, pl.ds(my_rows, rows), :], dst.at[:, pl.ds(col(b), TILE)], asem.at[k]).start()
                remote(src.at[b, pl.ds(other_rows, rows), :], dst.at[:, pl.ds(col(b), TILE)], asem.at[k + 1],
                       asem.at[k + 2], partner).start()
            o_copy(b).start()
            s_copy(b).start()

        @pl.loop(0, blocks)
        def _(b):
            o_copy(b).wait_recv()
            s_copy(b).wait_recv()
            far = jnp.concatenate([st_recv[b], jnp.zeros((HEAD - 8, HEAD), F32)], axis=0).T
            near = st_loc[b]
            for i in range(PER_BLOCK):
                at = pl.ds(i * HEAD, HEAD)
                m_a, l_a = near[:, 2 * i:2 * i + 1], near[:, 2 * i + 1:2 * i + 2]
                m_b, l_b = far[:, 2 * i:2 * i + 1], far[:, 2 * i + 1:2 * i + 2]
                peak = jnp.maximum(m_a, m_b)
                w_a, w_b = jnp.exp(m_a - peak), jnp.exp(m_b - peak)
                norm_l = 1.0 / (l_a * w_a + l_b * w_b)
                o = o_loc[b, :, at] * (w_a * norm_l) + o_recv[b, :, at] * (w_b * norm_l)
                obuf[:, pl.ds(pl.multiple_of(core * half + b * TILE + i * HEAD, 128), HEAD)] = o.astype(BF16)
            piece = obuf.at[:, pl.ds(col(b), TILE)]
            remote(piece, piece, dsend.at[0], drecv.at[0], partner).start()

        mine = obuf.at[:, pl.ds(my_cols, half)]
        theirs = obuf.at[:, pl.ds(other_cols, half)]
        remote(mine, theirs, dsend.at[0], drecv.at[0], partner).wait_send()
        remote(mine, theirs, dsend.at[0], drecv.at[0], partner).wait_recv()

        @pl.loop(0, blocks)
        def _(b):
            q_copy(b).wait_send()
            o_copy(b).wait_send()
            s_copy(b).wait_send()

        for dst, k in ((k_out, 0), (v_out, 3)):
            to_me = dst.at[:, pl.ds(my_cols, half)]
            to_me2 = dst.at[:, pl.ds(other_cols, half)]
            pltpu.make_async_copy(to_me, to_me, asem.at[k]).wait()
            remote(to_me, to_me2, asem.at[k + 1], asem.at[k + 2], partner).wait_send()
            remote(to_me, to_me2, asem.at[k + 1], asem.at[k + 2], partner).wait_recv()

    def both_wait(buf, sem, width, my_at, other_at):
        mine = buf.at[:, pl.ds(my_at, width)]
        theirs = buf.at[:, pl.ds(other_at, width)]
        remote(mine, theirs, dsend.at[sem], drecv.at[sem], partner).wait_send()
        remote(mine, theirs, dsend.at[sem], drecv.at[sem], partner).wait_recv()

    attention(xin, base1, 0, cache1, k1_out, v1_out)
    cache2 = cache_copies(ck2, cv2)
    for c in cache2:
        c.start()

    @pl.loop(0, blocks)
    def _(b):
        s = base1 + 3 * blocks + b
        slot = wait_tile(s)
        y = jnp.dot(obuf[...], wring[slot], preferred_element_type=F32).astype(BF16)
        start_tile(s + SLOTS, base1 + 3 * blocks + SLOTS, base_up + SLOTS)
        at = pl.ds(col(b), TILE)
        hbuf[:, at] = (xin[:, at].astype(F32) + y.astype(F32)).astype(BF16)
        remote(hbuf.at[:, at], hbuf.at[:, at], dsend.at[1], drecv.at[1], partner).start()

    both_wait(hbuf, 1, half, my_cols, other_cols)
    norm(hbuf)

    @pl.loop(0, ffn)
    def _(n):
        s = base_up + n
        slot = wait_tile(s)
        both = jnp.dot(nbuf[...], wring[slot], preferred_element_type=F32)
        start_tile(s + SLOTS, base_up + SLOTS, base_down + SLOTS)
        gate = both[:, :TILE // 2].astype(BF16).astype(F32)
        up = both[:, TILE // 2:].astype(BF16).astype(F32)
        at = pl.ds(pl.multiple_of(core * ffh + n * (TILE // 2), 128), TILE // 2)
        ebuf[:, at] = (jax.nn.silu(gate) * up).astype(BF16)
        remote(ebuf.at[:, at], ebuf.at[:, at], dsend.at[2], drecv.at[2], partner).start()

    both_wait(ebuf, 2, ffh, pl.multiple_of(core * ffh, 128), pl.multiple_of((1 - core) * ffh, 128))

    @pl.loop(0, blocks)
    def _(b):
        at = pl.ds(col(b), TILE)
        acc = hbuf[:, at].astype(F32)
        for k in range(3):
            s = base_down + 3 * b + k
            slot = wait_tile(s, ffc)
            part = jnp.dot(ebuf[:, k * ffc:(k + 1) * ffc], wring[slot, :ffc, :], preferred_element_type=F32)
            start_tile(s + SLOTS, base_down + k + SLOTS, base2 - 2 + k + SLOTS)
            down = part if k == 0 else down + part
        gbuf[:, at] = (acc + down).astype(BF16)
        remote(gbuf.at[:, at], gbuf.at[:, at], dsend.at[3], drecv.at[3], partner).start()

    both_wait(gbuf, 3, half, my_cols, other_cols)
    g_copy = pltpu.make_async_copy(gbuf.at[pl.ds(my_rows, rows), :], g_out, gsem.at[0])
    g_copy.start()
    norm(gbuf)

    attention(nbuf, base2, 2, cache2, k2_out, v2_out)

    @pl.loop(0, blocks)
    def _(b):
        s = base2 + 3 * blocks + b
        slot = wait_tile(s)
        ybuf[b] = jnp.dot(obuf[...], wring[slot], preferred_element_type=F32).astype(BF16)
        at = pl.ds(col(b), TILE)
        pltpu.make_async_copy(ybuf.at[b, pl.ds(my_rows, rows), :], y_out.at[:, at], gsem.at[1]).start()
        remote(ybuf.at[b, pl.ds(other_rows, rows), :], y_out.at[:, at], dsend.at[4], drecv.at[4], partner).start()

    y_mine = y_out.at[:, pl.ds(my_cols, half)]
    y_theirs = y_out.at[:, pl.ds(other_cols, half)]
    pltpu.make_async_copy(y_mine, y_mine, gsem.at[1]).wait()
    remote(y_mine, y_theirs, dsend.at[4], drecv.at[4], partner).wait_send()
    remote(y_mine, y_theirs, dsend.at[4], drecv.at[4], partner).wait_recv()
    g_copy.wait()


def solution(mesh):
    rows_spec = P(('dp', 'cp'), None)
    cache_spec = P(('dp', 'cp'), None, None)
    mat_spec = P(None, None)
    vec_spec = P(None)
    layer_specs = (cache_spec, cache_spec, mat_spec, vec_spec, mat_spec, vec_spec, mat_spec, mat_spec)
    in_specs = (rows_spec,) + layer_specs + (mat_spec, mat_spec, mat_spec) + layer_specs
    out_specs = (rows_spec, rows_spec, cache_spec, cache_spec, cache_spec, cache_spec)

    def forward(x_in, cache_k1, cache_v1, w_q1, b_q1, w_k1, b_k1, w_v1, w_o1, w_gate, w_up, w_down, cache_k2, cache_v2, w_q2, b_q2, w_k2, b_k2, w_v2, w_o2):
        rows, d_model = x_in.shape
        cache_rows, heads, head_dim = cache_k1.shape
        ff = w_gate.shape[1]
        half = d_model // 2
        blocks = half // TILE
        crows = 2 * rows
        first = 4 * cache_rows + (lax.axis_index('cp') // 2) * crows
        cos_t, sin_t = rope_tables(first + jnp.arange(crows), head_dim)
        bias = jnp.stack([b_q1, b_k1, b_q2, b_k2]).astype(F32)

        def flat(c):
            return c.reshape(cache_rows, d_model)

        any_spec = pl.BlockSpec(memory_space=pl.ANY)
        vmem_spec = pl.BlockSpec(memory_space=pltpu.VMEM)
        row_out = jax.ShapeDtypeStruct((rows, d_model), BF16)
        dma = pltpu.SemaphoreType.DMA
        out = pl.pallas_call(
            functools.partial(body, (d_model, ff, rows, cache_rows)),
            out_shape=[row_out] * 6,
            in_specs=[vmem_spec] * 3 + [any_spec] * 16,
            out_specs=[any_spec] * 6,
            scratch_shapes=[
                pltpu.VMEM((SLOTS, d_model, TILE), BF16),
                pltpu.VMEM((crows, d_model), BF16),
                pltpu.VMEM((crows, d_model), BF16),
                pltpu.VMEM((crows, d_model), BF16),
                pltpu.VMEM((crows, d_model), BF16),
                pltpu.VMEM((crows, ff), BF16),
                pltpu.VMEM((blocks, 2 * crows, TILE), BF16),
                pltpu.VMEM((blocks, crows, TILE), BF16),
                pltpu.VMEM((blocks, crows, TILE), BF16),
                pltpu.VMEM((2 * cache_rows, half), BF16),
                pltpu.VMEM((2 * cache_rows, half), BF16),
                pltpu.VMEM((blocks, crows, TILE), F32),
                pltpu.VMEM((blocks, crows, TILE), F32),
                pltpu.VMEM((blocks, crows, TILE), F32),
                pltpu.VMEM((crows, d_model), BF16),
                pltpu.VMEM((blocks, crows, TILE), BF16),
                pltpu.VMEM((blocks, crows, HEAD), F32),
                pltpu.VMEM((blocks, 8, HEAD), F32),
                pltpu.VMEM((blocks, 8, HEAD), F32),
                dma((SLOTS,)), dma((3,)), dma((6,)),
                dma((blocks,)), dma((blocks,)), dma((blocks,)), dma((blocks,)), dma((blocks,)), dma((blocks,)),
                dma((5,)), dma((5,)), dma((6,)), dma((2,)),
            ],
            compiler_params=pltpu.CompilerParams(
                collective_id=0, has_side_effects=True, vmem_limit_bytes=67043328),
        )(cos_t, sin_t, bias, x_in, flat(cache_k1), flat(cache_v1), flat(cache_k2), flat(cache_v2),
          w_q1, w_k1, w_v1, w_o1, w_gate, w_up, w_down, w_q2, w_k2, w_v2, w_o2)
        g, y2, k1, v1, k2, v2 = out

        def heads_of(a):
            return a.reshape(rows, heads, head_dim)

        return g, y2, heads_of(k1), heads_of(v1), heads_of(k2), heads_of(v2)

    return jax.shard_map(forward, mesh=mesh, in_specs=in_specs, out_specs=out_specs, check_vma=False)
```

time: 829 us -> 204 us (0.25)
  matrix products: 364 us -> 0 us
  waiting for transfers between devices: 348 us -> 0 us
  Pallas kernels: 0 us -> 181 us
  local copies, waits for them, and re-layouts: 67.2 us -> 20.4 us
  other arithmetic: 22.5 us -> 1.82 us
  between operations: 14.7 us -> 0.72 us
    dot_general x31 -> x0, matrix products: 364 us -> none  [the longest x1 49 us: mlp_block(): jnp.dot(normed, w_up, preferred_element_type=jnp.float32)]
    ppermute x12 -> x0, waiting for transfers between devices: 330 us -> none  [the longest x6 184 us: cache_step(): blk_k = lax.ppermute(blk_k, 'cp', shift)]
    pallas_call x0 -> x1, Pallas kernels: none -> 181 us  [forward(): pl.pallas_call(functools.partial(body, (d_model, ff, rows, cache_rows)),...]
    while x40 -> x0, local copies, waits for them, and re-layouts: 46.4 us -> none
    all_gather x4 -> x0, waiting for transfers between devices: 17.7 us -> none  [the longest x2 17.6 us: attention_layer(): all_v = lax.all_gather(v_new, 'cp', axis=0, tiled=True)]
    reduce_sum x10 -> x0, other arithmetic: 9.69 us -> none  [partial_attend(): total = jnp.sum(prob_w, axis=-1)]
  transfers between devices with their start and end apart: 16 -> 0, of which waited for: 14 -> 0; matrix products, arithmetic and copies ran while one was open for 12% -> 0% of each run, Pallas kernels for 0% -> 0%
where the time goes in v1:
time: 204 us
  Pallas kernels  181 us (89%)
  local copies, waits for them, and re-layouts  20.4 us (10%)
    pallas_call x1, Pallas kernels, forward(): pl.pallas_call(functools.partial(body, (d_model, ff, rows, cache_rows)),...  181 us
    reshape x2, local copies, waits for them, and re-layouts, flat(): return c.reshape(cache_rows, d_model)  9.69 us
    unnamed x18, local copies, waits for them, and re-layouts  7.85 us

profile of v1, /device:TPU:0, one launch (start us, length us, event | category | flops | bytes accessed | tf_op | source)
XLA Modules:
  0.0 203.6 jit_solution(8876301629321565894)
XLA Ops:
  0.7 0.7 stack.15
  1.4 0.7 stack.16
  2.1 0.7 stack.17
  2.8 0.7 stack.18
  3.6 0.7 maximum_convert_fusion.bias_ref
  4.3 0.3 fusion
  4.6 0.8 pad_maximum_fusion
  5.4 0.0 copy-start
  5.4 0.0 copy-start.1
  5.4 6.2 %copy_bitcast_fusion.2 = (bf16[256,5120]{1,0:T(8,128)(2,1)}, bf16[256,5120]{1,0:T(8,128)(2,1)}) fusion(bf16[32,8,40,128]{3,2,1,0:T(8,128)(2,1)} %bitcast.20, bf16[32,8,40,128]{3,2,1,0:T(8,128)(2,1)} %bitcast.21), kind=kLoop, calls=%fused_computation.2 | loop fusion | bytes 10485760 | tf_op jit(solution)/shard_map/reshape | solution.py:381
  11.5 0.0 copy-done
  11.5 0.0 copy-done.1
  11.5 3.5 %copy_bitcast_fusion = (bf16[256,5120]{1,0:T(8,128)(2,1)}, bf16[256,5120]{1,0:T(8,128)(2,1)}) fusion(bf16[32,8,40,128]{3,2,1,0:T(8,128)(2,1)S(1)} %bitcast.22, bf16[32,8,40,128]{3,2,1,0:T(8,128)(2,1)S(1)} %bitcast.23), kind=kLoop, calls=%fused_computation | loop fusion | bytes 10485760 | tf_op jit(solution)/shard_map/reshape | solution.py:381
  15.1 180.7 %shard_map.235 = (bf16[64,5120]{1,0:T(8,128)(2,1)}, bf16[64,5120]{1,0:T(8,128)(2,1)}, bf16[64,5120]{1,0:T(8,128)(2,1)}, bf16[64,5120]{1,0:T(8,128)(2,1)}, bf16[6...) custom-call(f32[128,128]{1,0:T(8,128)} %get-tuple-element.21.cos_ref, f32[128,128]{1,0:T(8,128)} %get-tuple-element.22.sin_ref, ...), custom_call_target="tpu_custom_call" | custom-call | tf_op jit(solution)/shard_map/pallas_call | solution.py:387
  195.7 0.0 copy-start.5
  195.8 0.0 copy-start.4
  195.8 0.0 copy-start.3
  195.8 2.2 %copy.30 = bf16[8,8,40,128]{3,2,1,0:T(8,128)(2,1)} copy(bf16[8,8,40,128]{3,1,2,0:T(8,128)(2,1)} %bitcast.31) | data formatting | bytes 1310720
  197.9 0.0 copy-start.2
  197.9 2.1 %copy.31 = bf16[8,8,40,128]{3,2,1,0:T(8,128)(2,1)} copy(bf16[8,8,40,128]{3,1,2,0:T(8,128)(2,1)} %bitcast.30) | data formatting | bytes 1310720
  200.0 0.0 copy-done.5
  200.0 0.9 copy.32
  201.0 0.0 copy-done.4
  201.0 0.9 copy.33
  201.9 0.0 copy-done.3
  201.9 0.8 copy.40
  202.8 0.0 copy-done.2
  202.8 0.8 copy.41
  (2 shorter events, 0.0 us)
Async XLA Ops:
  5.4 6.2 %copy-start = (bf16[256,40,128]{2,1,0:T(8,128)(2,1)S(1)}, bf16[256,40,128]{2,1,0:T(8,128)(2,1)}, u32[]{:S(2)}) copy-start(bf16[256,40,128]{2,1,0:T(8,128)(2,1)} %param.33) | copy-start | bytes 7864324
  5.4 6.2 %copy-start.1 = (bf16[256,40,128]{2,1,0:T(8,128)(2,1)S(1)}, bf16[256,40,128]{2,1,0:T(8,128)(2,1)}, u32[]{:S(2)}) copy-start(bf16[256,40,128]{2,1,0:T(8,128)(2,1)} %param.32) | copy-start | bytes 7864324
  195.7 4.3 %copy-start.5 = (bf16[64,5120]{1,0:T(8,128)(2,1)S(1)}, bf16[64,5120]{1,0:T(8,128)(2,1)}, u32[]{:S(2)}) copy-start(bf16[64,5120]{1,0:T(8,128)(2,1)} %get-tuple-element.16) | copy-start | bytes 1966084
  195.8 5.2 %copy-start.4 = (bf16[64,5120]{1,0:T(8,128)(2,1)S(1)}, bf16[64,5120]{1,0:T(8,128)(2,1)}, u32[]{:S(2)}) copy-start(bf16[64,5120]{1,0:T(8,128)(2,1)} %get-tuple-element.17) | copy-start | bytes 1966084
  195.8 6.2 %copy-start.3 = (bf16[64,5120]{1,0:T(8,128)(2,1)S(1)}, bf16[64,5120]{1,0:T(8,128)(2,1)}, u32[]{:S(2)}) copy-start(bf16[64,5120]{1,0:T(8,128)(2,1)} %get-tuple-element.33) | copy-start | bytes 1966084
  197.9 4.8 %copy-start.2 = (bf16[64,5120]{1,0:T(8,128)(2,1)S(1)}, bf16[64,5120]{1,0:T(8,128)(2,1)}, u32[]{:S(2)}) copy-start(bf16[64,5120]{1,0:T(8,128)(2,1)} %get-tuple-element.34) | copy-start | bytes 1966084

commit v2 on v1

--- a/solution.py
+++ b/solution.py
@@ -2,6 +2,7 @@
 
 import jax
 import jax.numpy as jnp
+import numpy as np
 from jax import lax
 from jax.experimental import pallas as pl
 from jax.experimental.pallas import tpu as pltpu
@@ -21,17 +22,18 @@
 
 def rope_tables(positions, head_dim):
     half_dim = head_dim // 2
-    inv_freq = 1.0 / (ROPE_THETA ** (jnp.arange(half_dim, dtype=F32) * (2.0 / head_dim)))
-    angles = positions.astype(F32)[:, None] * inv_freq[None, :]
-    cos_t, sin_t = jnp.cos(angles), jnp.sin(angles)
-    return jnp.concatenate([cos_t, cos_t], axis=1), jnp.concatenate([-sin_t, sin_t], axis=1)
-
-
-def body(dims, cos_ref, sin_ref, bias_ref, x_hbm, ck1, cv1, ck2, cv2, wq1, wk1, wv1, wo1, w_gate, w_up, w_down,
+    inv_freq = (1.0 / (ROPE_THETA ** (np.arange(half_dim, dtype=np.float32) * np.float32(2.0 / head_dim)))).astype(np.float32)
+    angles = positions.astype(np.float32)[:, None] * inv_freq[None, :]
+    cos_t, sin_t = np.cos(angles), np.sin(angles)
+    return np.concatenate([cos_t, cos_t], axis=1), np.concatenate([-sin_t, sin_t], axis=1)
+
+
+def body(dims, cos_ref, sin_ref, bq1, bk1, bq2, bk2, x_hbm, ck1, cv1, ck2, cv2, wq1, wk1, wv1, wo1, w_gate, w_up, w_down,
          wq2, wk2, wv2, wo2, g_out, y_out, k1_out, v1_out, k2_out, v2_out,
-         wring, xin, hbuf, nbuf, gbuf, ebuf, qcat, knew, vnew, kc, vc, o_loc, o_send, o_recv, obuf, ybuf,
-         st_loc, st_send, st_recv,
-         wsem, xsem, csem, qsend, qrecv, osend, orecv, ssend, srecv, dsend, drecv, asem, gsem):
+         wring, nbuf, gbuf, ebuf, pre, kc, vc, o_loc, o_send, o_recv, obuf, opair,
+         st_loc, st_send, st_recv, bias32,
+         wsem, xsem, csem, c2send, c2recv, qsend, qrecv, osend, orecv, ssend, srecv, dsend, drecv, asem, gsem,
+         gxs, gxr, a2send, a2recv):
     d_model, ff, rows, cache_rows = dims
     half = d_model // 2
     ffh = ff // 2
@@ -39,11 +41,17 @@
     blocks = half // TILE
     ffn = ffh // (TILE // 2)
     crows = 2 * rows
+    quart = half // 2
+    ybuf = nbuf.at[pl.ds(0, rows), :]
     me = lax.axis_index("cp")
     core = lax.rem(me, 2)
     chip = me // 2
     partner = me + 1 - 2 * core
     peer = lax.rem(me + 2, 4)
+    diag = 3 - me
+    chip_rows = pl.multiple_of(chip * crows, 16)
+    xin = hbuf = gbuf.at[pl.ds(pl.multiple_of(chip * crows, 16), crows), :]
+    far_rows = pl.multiple_of((1 - chip) * crows, 16)
     my_cols = pl.multiple_of(core * half, 128)
     my_rows = pl.multiple_of(core * rows, 16)
     other_rows = pl.multiple_of((1 - core) * rows, 16)
@@ -57,7 +65,7 @@
     base_up = attn_tiles
     base_down = base_up + ffn
     base2 = base_down + 3 * blocks
-    total = base2 + attn_tiles
+    qkv2 = 8
 
     def start_full(w, b, slot):
         pltpu.make_async_copy(w.at[:, pl.ds(col(b), TILE)], wring.at[slot], wsem.at[slot]).start()
@@ -85,10 +93,39 @@
             (base + loop_end + 2, base + attn_tiles, lambda r, slot: start_full(wo, r, slot), None),
         ]
 
+    PAIR = TILE // 2
+    own2 = core * half + chip * quart
+
+    def start_v2(t, slot):
+        @pl.when(t < qkv2 - 2)
+        def _():
+            pltpu.make_async_copy(wv2.at[:, pl.ds(pl.multiple_of(own2 + (t // 3) * TILE, 128), TILE)], wring.at[slot],
+                                  wsem.at[slot]).start()
+
+        @pl.when(t >= qkv2 - 2)
+        def _():
+            pltpu.make_async_copy(wv2.at[:, pl.ds(pl.multiple_of(own2 + (t // 3) * TILE, 128), PAIR)],
+                                  wring.at[slot, :, pl.ds(0, PAIR)], wsem.at[slot]).start()
+
+    def start_qk2(t, slot):
+        at = pl.ds(pl.multiple_of(own2 + (t - 1 - t // 3) * PAIR, 128), PAIR)
+        pltpu.make_async_copy(wq2.at[:, at], wring.at[slot, :, pl.ds(0, PAIR)], wsem.at[slot]).start()
+        pltpu.make_async_copy(wk2.at[:, at], wring.at[slot, :, pl.ds(PAIR, PAIR)], wsem.at[slot]).start()
+
+    def start_wo2(b, slot):
+        for i in range(2):
+            pltpu.make_async_copy(
+                wo2.at[pl.ds(my_cols, half), pl.ds(pl.multiple_of(b * 2 * TILE + i * TILE, 128), TILE)],
+                wring.at[slot, pl.ds(i * half, half), :], wsem.at[slot]).start()
+
     segments = attn_segments(base1, wq1, wk1, wv1, wo1) + [
         (base_up, base_down, start_mlp, None),
         (base_down, base2, start_down, None),
-    ] + attn_segments(base2, wq2, wk2, wv2, wo2)
+        (base2, base2 + qkv2, start_v2, 0),
+        (base2, base2 + qkv2, start_qk2, 1),
+        (base2, base2 + qkv2, start_qk2, 2),
+        (base2 + qkv2, base2 + qkv2 + blocks, start_wo2, None),
+    ]
 
     def start_tile(s, lo, hi):
         slot = lax.rem(s, SLOTS) if not isinstance(s, int) else s % SLOTS
@@ -121,9 +158,9 @@
         start_tile(s, s, s + 1)
 
     barrier = pltpu.get_barrier_semaphore()
-    for who in (partner, peer):
+    for who in (partner, peer, diag):
         pl.semaphore_signal(barrier, inc=1, device_id={"cp": who}, device_id_type=MESH)
-    pl.semaphore_wait(barrier, 2)
+    pl.semaphore_wait(barrier, 3)
 
     x_loc = pltpu.make_async_copy(x_hbm, xin.at[pl.ds(my_rows, rows)], xsem.at[0])
     x_rem = remote(x_hbm, xin.at[pl.ds(my_rows, rows)], xsem.at[1], xsem.at[2], partner)
@@ -142,24 +179,28 @@
     cache1 = cache_copies(ck1, cv1)
     for c in cache1:
         c.start()
+    for i, ref in enumerate((bq1, bk1, bq2, bk2)):
+        bias32[i] = ref[...].astype(F32)
     x_loc.wait()
     x_rem.wait()
 
-    def rope(vals):
+    def biased_rope(vals, bias_row, first_head, table_at, n):
         parts = []
-        for i in range(PER_BLOCK):
-            seg = vals[:, i * HEAD:(i + 1) * HEAD]
-            parts.append(seg * cos_ref[...] + pltpu.roll(seg, HEAD // 2, 1) * sin_ref[...])
+        cos_t, sin_t = cos_ref[table_at, :], sin_ref[table_at, :]
+        for i in range(n):
+            seg = vals[:, i * HEAD:(i + 1) * HEAD] + bias32[bias_row, pl.ds(first_head + i, 1), :]
+            seg = seg.astype(BF16).astype(F32)
+            parts.append((seg * cos_t + pltpu.roll(seg, HEAD // 2, 1) * sin_t).astype(BF16))
         return jnp.concatenate(parts, axis=1)
 
-    def norm(src):
+    def norm(src, dst, first, count):
         step = 16
 
-        @pl.loop(0, crows // step)
+        @pl.loop(0, count // step)
         def _(i):
-            at = pl.ds(pl.multiple_of(i * step, step), step)
+            at = pl.ds(pl.multiple_of(first + i * step, step), step)
             wide = src[at, :].astype(F32)
-            nbuf[at, :] = (wide * lax.rsqrt(jnp.mean(wide * wide, axis=-1, keepdims=True) + NORM_EPS)).astype(BF16)
+            dst[at, :] = (wide * lax.rsqrt(jnp.mean(wide * wide, axis=-1, keepdims=True) + NORM_EPS)).astype(BF16)
 
     row_i = lax.broadcasted_iota(jnp.int32, (2 * crows, crows), 0)
     col_i = lax.broadcasted_iota(jnp.int32, (2 * crows, crows), 1)
@@ -174,16 +215,16 @@
         for i in range(PER_BLOCK):
             at = pl.ds(i * HEAD, HEAD)
             cat = pl.ds(pl.multiple_of(b * TILE + i * HEAD, 128), HEAD)
-            q = qcat[b, :, at]
+            q = pre[b, :, at]
             s_old = lax.dot_general(q, kc[:, cat], dims_t, preferred_element_type=F32) * scale
-            s_new = lax.dot_general(q, knew[b, :, at], dims_t, preferred_element_type=F32) * scale
+            s_new = lax.dot_general(q, pre[blocks + b, pl.ds(0, crows), at], dims_t, preferred_element_type=F32) * scale
             s_new = jnp.where(visible, s_new, -jnp.inf)
             peak = jnp.maximum(jnp.max(s_old, axis=1, keepdims=True), jnp.max(s_new, axis=1, keepdims=True))
             p_old = jnp.exp(s_old - peak)
             p_new = jnp.exp(s_new - peak)
             total_p = jnp.sum(p_old, axis=1, keepdims=True) + jnp.sum(p_new, axis=1, keepdims=True)
             acc = jnp.dot(p_old.astype(BF16), vc[:, cat], preferred_element_type=F32)
-            acc = acc + jnp.dot(p_new.astype(BF16), vnew[b, :, at], preferred_element_type=F32)
+            acc = acc + jnp.dot(p_new.astype(BF16), pre[blocks + b, pl.ds(crows, crows), at], preferred_element_type=F32)
             o_loc[b, :, at] = acc[:crows]
             o_send[b, :, at] = acc[crows:]
             stats = jnp.where(lane == 2 * i, peak, stats)
@@ -192,21 +233,23 @@
         st_send[b] = stats[crows:].T[:8, :]
 
     def q_copy(b):
-        return remote(qcat.at[b, pl.ds(0, crows), :], qcat.at[b, pl.ds(crows, crows), :], qsend.at[b], qrecv.at[b], peer)
+        return remote(pre.at[b, pl.ds(0, crows), :], pre.at[b, pl.ds(crows, crows), :], qsend.at[b], qrecv.at[b], peer)
 
     def o_copy(b):
         return remote(o_send.at[b], o_recv.at[b], osend.at[b], orecv.at[b], peer)
 
     def s_copy(b):
         return remote(st_send.at[b], st_recv.at[b], ssend.at[b], srecv.at[b], peer)
+
+    def head_of(b):
+        return core * (half // HEAD) + b * PER_BLOCK
 
     def attention(layer_in, base, bias_row, caches, k_out, v_out):
         def q_step(b, s, lo, hi):
             slot = wait_tile(s)
-            pre = (jnp.dot(layer_in[...], wring[slot], preferred_element_type=F32)
-                   + bias_ref[pl.ds(bias_row, 1), pl.ds(col(b), TILE)]).astype(BF16)
+            raw = jnp.dot(layer_in[...], wring[slot], preferred_element_type=F32)
             start_tile(s + SLOTS, lo + SLOTS, hi + SLOTS)
-            qcat[b, pl.ds(0, crows), :] = rope(pre.astype(F32)).astype(BF16)
+            pre[b, pl.ds(0, crows), :] = biased_rope(raw, bias_row, head_of(b), pl.ds(chip_rows, crows), PER_BLOCK)
             q_copy(b).start()
 
         q_step(0, base, base, base + 1)
@@ -222,15 +265,14 @@
 
             s = s + has_q
             slot = wait_tile(s)
-            pre = (jnp.dot(layer_in[...], wring[slot], preferred_element_type=F32)
-                   + bias_ref[pl.ds(bias_row + 1, 1), pl.ds(col(b), TILE)]).astype(BF16)
+            raw = jnp.dot(layer_in[...], wring[slot], preferred_element_type=F32)
             start_tile(s + SLOTS, base + 2 + SLOTS, base + loop_end + 2 + SLOTS)
-            knew[b] = rope(pre.astype(F32)).astype(BF16)
+            pre[blocks + b, pl.ds(0, crows), :] = biased_rope(raw, bias_row + 1, head_of(b), pl.ds(chip_rows, crows), PER_BLOCK)
             s = s + 1
             slot = wait_tile(s)
             vals = jnp.dot(layer_in[...], wring[slot], preferred_element_type=F32).astype(BF16)
             start_tile(s + SLOTS, base + 3 + SLOTS, base + loop_end + 2 + SLOTS)
-            vnew[b] = vals
+            pre[blocks + b, pl.ds(crows, crows), :] = vals
 
             @pl.when(b == 0)
             def _():
@@ -239,9 +281,9 @@
 
             q_copy(b).wait_recv()
             attend(b)
-            for src, dst, k in ((knew, k_out, 0), (vnew, v_out, 3)):
-                pltpu.make_async_copy(src.at[b, pl.ds(my_rows, rows), :], dst.at[:, pl.ds(col(b), TILE)], asem.at[k]).start()
-                remote(src.at[b, pl.ds(other_rows, rows), :], dst.at[:, pl.ds(col(b), TILE)], asem.at[k + 1],
+            for part, dst, k in ((0, k_out, 0), (crows, v_out, 3)):
+                pltpu.make_async_copy(pre.at[blocks + b, pl.ds(part + my_rows, rows), :], dst.at[:, pl.ds(col(b), TILE)], asem.at[k]).start()
+                remote(pre.at[blocks + b, pl.ds(part + other_rows, rows), :], dst.at[:, pl.ds(col(b), TILE)], asem.at[k + 1],
                        asem.at[k + 2], partner).start()
             o_copy(b).start()
             s_copy(b).start()
@@ -289,9 +331,21 @@
         remote(mine, theirs, dsend.at[sem], drecv.at[sem], partner).wait_recv()
 
     attention(xin, base1, 0, cache1, k1_out, v1_out)
-    cache2 = cache_copies(ck2, cv2)
-    for c in cache2:
-        c.start()
+
+    def cache2_copy(kv, kind):
+        src, dst = ((ck2, kc), (cv2, vc))[kv]
+        who, to_core, to_chip = ((None, core, chip), (partner, 1 - core, chip), (peer, core, 1 - chip),
+                                 (diag, 1 - core, 1 - chip))[kind]
+        side = 0 if kind < 2 else quart
+        from_at = pl.ds(pl.multiple_of(to_core * half + to_chip * quart, 128), quart)
+        to = dst.at[pl.ds(pl.multiple_of(core * cache_rows, 16), cache_rows), pl.ds(side, quart)]
+        if kind == 0:
+            return pltpu.make_async_copy(src.at[:, from_at], to, c2send.at[4 * kv])
+        return remote(src.at[:, from_at], to, c2send.at[4 * kv + kind], c2recv.at[4 * kv + kind], who)
+
+    for kind in (2, 3, 1, 0):
+        for kv in range(2):
+            cache2_copy(kv, kind).start()
 
     @pl.loop(0, blocks)
     def _(b):
@@ -304,13 +358,13 @@
         remote(hbuf.at[:, at], hbuf.at[:, at], dsend.at[1], drecv.at[1], partner).start()
 
     both_wait(hbuf, 1, half, my_cols, other_cols)
-    norm(hbuf)
+    norm(hbuf, nbuf, 0, crows)
 
     @pl.loop(0, ffn)
     def _(n):
         s = base_up + n
         slot = wait_tile(s)
-        both = jnp.dot(nbuf[...], wring[slot], preferred_element_type=F32)
+        both = jnp.dot(nbuf[pl.ds(0, crows), :], wring[slot], preferred_element_type=F32)
         start_tile(s + SLOTS, base_up + SLOTS, base_down + SLOTS)
         gate = both[:, :TILE // 2].astype(BF16).astype(F32)
         up = both[:, TILE // 2:].astype(BF16).astype(F32)
@@ -319,6 +373,9 @@
         remote(ebuf.at[:, at], ebuf.at[:, at], dsend.at[2], drecv.at[2], partner).start()
 
     both_wait(ebuf, 2, ffh, pl.multiple_of(core * ffh, 128), pl.multiple_of((1 - core) * ffh, 128))
+
+    def g_piece(b, first):
+        return gbuf.at[pl.ds(first, crows), pl.ds(col(b), TILE)]
 
     @pl.loop(0, blocks)
     def _(b):
@@ -330,30 +387,180 @@
             part = jnp.dot(ebuf[:, k * ffc:(k + 1) * ffc], wring[slot, :ffc, :], preferred_element_type=F32)
             start_tile(s + SLOTS, base_down + k + SLOTS, base2 - 2 + k + SLOTS)
             down = part if k == 0 else down + part
-        gbuf[:, at] = (acc + down).astype(BF16)
-        remote(gbuf.at[:, at], gbuf.at[:, at], dsend.at[3], drecv.at[3], partner).start()
-
-    both_wait(gbuf, 3, half, my_cols, other_cols)
-    g_copy = pltpu.make_async_copy(gbuf.at[pl.ds(my_rows, rows), :], g_out, gsem.at[0])
+        gbuf[pl.ds(chip_rows, crows), at] = (acc + down).astype(BF16)
+        piece = g_piece(b, chip_rows)
+        remote(piece, piece, gxs.at[b], gxr.at[b], peer).start()
+        remote(piece, piece, dsend.at[3], drecv.at[3], partner).start()
+
+    def g_wait(first, sem):
+        mine = gbuf.at[pl.ds(first, crows), pl.ds(my_cols, half)]
+        theirs = gbuf.at[pl.ds(first, crows), pl.ds(other_cols, half)]
+        remote(mine, theirs, dsend.at[sem], drecv.at[sem], partner).wait_send()
+        remote(mine, theirs, dsend.at[sem], drecv.at[sem], partner).wait_recv()
+
+    g_wait(chip_rows, 3)
+    g_copy = pltpu.make_async_copy(gbuf.at[pl.ds(pl.multiple_of(chip_rows + my_rows, 16), rows), :], g_out, gsem.at[0])
     g_copy.start()
-    norm(gbuf)
-
-    attention(nbuf, base2, 2, cache2, k2_out, v2_out)
+    norm(gbuf, nbuf, chip_rows, crows)
 
     @pl.loop(0, blocks)
     def _(b):
-        s = base2 + 3 * blocks + b
-        slot = wait_tile(s)
-        ybuf[b] = jnp.dot(obuf[...], wring[slot], preferred_element_type=F32).astype(BF16)
-        at = pl.ds(col(b), TILE)
-        pltpu.make_async_copy(ybuf.at[b, pl.ds(my_rows, rows), :], y_out.at[:, at], gsem.at[1]).start()
-        remote(ybuf.at[b, pl.ds(other_rows, rows), :], y_out.at[:, at], dsend.at[4], drecv.at[4], partner).start()
-
-    y_mine = y_out.at[:, pl.ds(my_cols, half)]
-    y_theirs = y_out.at[:, pl.ds(other_cols, half)]
-    pltpu.make_async_copy(y_mine, y_mine, gsem.at[1]).wait()
-    remote(y_mine, y_theirs, dsend.at[4], drecv.at[4], partner).wait_send()
-    remote(y_mine, y_theirs, dsend.at[4], drecv.at[4], partner).wait_recv()
+        far = g_piece(b, far_rows)
+        remote(far, far, gxs.at[b], gxr.at[b], peer).wait_recv()
+        remote(far, far, dsend.at[0], drecv.at[0], partner).start()
+
+    g_wait(far_rows, 0)
+    norm(gbuf, nbuf, far_rows, crows)
+
+    heads2 = quart // HEAD
+    row_2 = lax.broadcasted_iota(jnp.int32, (2 * crows, 2 * crows), 0)
+    col_2 = lax.broadcasted_iota(jnp.int32, (2 * crows, 2 * crows), 1)
+
+    def qk_tile(b):
+        return b + 1 + b // 2
+
+    def attend2(b):
+        t = qk_tile(b)
+        vt = 3 * (b // 2)
+        dims_t = (((1,), (1,)), ((), ()))
+        visible = col_2 <= row_2
+        for i in range(2):
+            near = pl.ds(pl.multiple_of(b * PAIR + i * HEAD, 128), HEAD)
+            far = pl.ds(pl.multiple_of(quart + b * PAIR + i * HEAD, 128), HEAD)
+            v_at = pl.ds(pl.multiple_of(lax.rem(b, 2) * PAIR + i * HEAD, 128), HEAD)
+            q = pre[t, :, pl.ds(i * HEAD, HEAD)]
+            s_a = lax.dot_general(q, kc[:, near], dims_t, preferred_element_type=F32) * scale
+            s_b = lax.dot_general(q, kc[:, far], dims_t, preferred_element_type=F32) * scale
+            s_n = lax.dot_general(q, pre[t, :, pl.ds(PAIR + i * HEAD, HEAD)], dims_t, preferred_element_type=F32) * scale
+            s_n = jnp.where(visible, s_n, -jnp.inf)
+            peak = jnp.maximum(jnp.maximum(jnp.max(s_a, axis=1, keepdims=True), jnp.max(s_b, axis=1, keepdims=True)),
+                               jnp.max(s_n, axis=1, keepdims=True))
+            p_a, p_b, p_n = jnp.exp(s_a - peak), jnp.exp(s_b - peak), jnp.exp(s_n - peak)
+            total_p = (jnp.sum(p_a, axis=1, keepdims=True) + jnp.sum(p_b, axis=1, keepdims=True)
+                       + jnp.sum(p_n, axis=1, keepdims=True))
+            acc = jnp.dot(p_a.astype(BF16), vc[:, near], preferred_element_type=F32)
+            acc = acc + jnp.dot(p_b.astype(BF16), vc[:, far], preferred_element_type=F32)
+            acc = acc + jnp.dot(p_n.astype(BF16), pre[vt, :, v_at], preferred_element_type=F32)
+            opair[:, pl.ds(i * HEAD, HEAD)] = (acc * (1.0 / total_p)).astype(BF16)
+
+    def o2_piece(b, from_chip):
+        return obuf.at[:, pl.ds(pl.multiple_of(from_chip * quart + b * PAIR, 128), PAIR)]
+
+    def o2_far(b):
+        return obuf.at[:, pl.ds(pl.multiple_of(half + b * PAIR, 128), PAIR)]
+
+    def o2_copy(b):
+        return remote(o2_far(b), o2_piece(b, chip), osend.at[b], orecv.at[b], peer)
+
+    def append2(b, kind):
+        who, to_core, to_chip = ((None, core, chip), (partner, 1 - core, chip), (peer, core, 1 - chip),
+                                 (diag, 1 - core, 1 - chip))[kind]
+        row_at = pl.ds(pl.multiple_of(to_chip * crows + to_core * rows, 16), rows)
+        to_at = pl.ds(pl.multiple_of(own2 + b * PAIR, 128), PAIR)
+        v_at = pl.ds(pl.multiple_of(lax.rem(b, 2) * PAIR, 128), PAIR)
+        for kv, (part, dst) in enumerate(((pre.at[qk_tile(b), row_at, pl.ds(PAIR, PAIR)], k2_out),
+                                          (pre.at[3 * (b // 2), row_at, v_at], v2_out))):
+            if kind == 0:
+                pltpu.make_async_copy(part, dst.at[:, to_at], a2send.at[4 * kv]).start()
+            else:
+                remote(part, dst.at[:, to_at], a2send.at[4 * kv + kind], a2recv.at[4 * kv + kind], who).start()
+
+    early = 2
+
+    @pl.loop(0, qkv2)
+    def _(t):
+        s = base2 + t
+
+        @pl.when(t == qkv2 - 2)
+        def _():
+            at = wring.at[lax.rem(s, SLOTS), :, pl.ds(0, PAIR)]
+            pltpu.make_async_copy(at, at, wsem.at[lax.rem(s, SLOTS)]).wait()
+
+        @pl.when(t != qkv2 - 2)
+        def _():
+            wait_tile(s)
+
+        raw = jnp.dot(nbuf[...], wring[lax.rem(s, SLOTS)], preferred_element_type=F32)
+        start_tile(s + SLOTS, base2 + SLOTS, base2 + qkv2 + SLOTS)
+
+        @pl.when(lax.rem(t, 3) == 0)
+        def _():
+            pre[t] = raw.astype(BF16)
+
+        @pl.when(lax.rem(t, 3) != 0)
+        def _():
+            b = t - 1 - t // 3
+            head = own2 // HEAD + 2 * b
+            all_rows = pl.ds(0, 2 * crows)
+            pre[t, :, pl.ds(0, PAIR)] = biased_rope(raw[:, :PAIR], 2, head, all_rows, 2)
+            pre[t, :, pl.ds(PAIR, PAIR)] = biased_rope(raw[:, PAIR:], 3, head, all_rows, 2)
+
+            @pl.when(b == 0)
+            def _():
+                for kv in range(2):
+                    for kind in range(4):
+                        cache2_copy(kv, kind).wait()
+
+            attend2(b)
+            obuf[:, pl.ds(pl.multiple_of(chip * quart + b * PAIR, 128), PAIR)] = opair[pl.ds(chip_rows, crows), :]
+            obuf[:, pl.ds(pl.multiple_of(half + b * PAIR, 128), PAIR)] = opair[pl.ds(far_rows, crows), :]
+            o2_copy(b).start()
+            append2(b, 0)
+            append2(b, 1)
+
+            @pl.when(b < early)
+            def _():
+                append2(b, 2)
+                append2(b, 3)
+
+    @pl.loop(early, blocks)
+    def _(b):
+        append2(b, 2)
+        append2(b, 3)
+
+    @pl.loop(0, blocks)
+    def _(b):
+        remote(o2_far(b), o2_piece(b, 1 - chip), osend.at[b], orecv.at[b], peer).wait_recv()
+
+    def y_copy(b):
+        return remote(o_send.at[b], o_recv.at[b], qsend.at[b], qrecv.at[b], partner)
+
+    @pl.loop(0, blocks)
+    def _(b):
+        slot = wait_tile(base2 + qkv2 + b)
+        for i in range(2):
+            y = jnp.dot(obuf[:, :half], wring[slot, i * half:(i + 1) * half, :], preferred_element_type=F32)
+            at = pl.ds(i * rows, rows)
+            for j in range(PER_BLOCK):
+                lanes = pl.ds(j * HEAD, HEAD)
+                st_loc[j] = y[:, j * HEAD:(j + 1) * HEAD]
+                o_send[b, at, lanes] = st_loc[j, pl.ds(other_rows, rows), :]
+                o_loc[b, at, lanes] = st_loc[j, pl.ds(my_rows, rows), :]
+        y_copy(b).start()
+
+    @pl.loop(0, blocks)
+    def _(b):
+        y_copy(b).wait_recv()
+        for i in range(2):
+            at = pl.ds(i * rows, rows)
+            ybuf[:, pl.ds(pl.multiple_of(b * 2 * TILE + i * TILE, 128), TILE)] = (o_loc[b, at, :] + o_recv[b, at, :]).astype(BF16)
+
+    y_copy_out = pltpu.make_async_copy(ybuf, y_out, gsem.at[1])
+    y_copy_out.start()
+
+    @pl.loop(0, blocks)
+    def _(b):
+        y_copy(b).wait_send()
+        o2_copy(b).wait_send()
+        remote(g_piece(b, chip_rows), g_piece(b, chip_rows), gxs.at[b], gxr.at[b], peer).wait_send()
+
+    for kv, dst in enumerate((k2_out, v2_out)):
+        ref = dst.at[:, pl.ds(0, quart)]
+        pltpu.make_async_copy(ref, ref, a2send.at[4 * kv]).wait()
+        for kind, who in ((1, partner), (2, peer), (3, diag)):
+            remote(ref, ref, a2send.at[4 * kv + kind], a2recv.at[4 * kv + kind], who).wait_send()
+            remote(ref, ref, a2send.at[4 * kv + kind], a2recv.at[4 * kv + kind], who).wait_recv()
+    y_copy_out.wait()
     g_copy.wait()
 
 
@@ -373,9 +580,8 @@
         half = d_model // 2
         blocks = half // TILE
         crows = 2 * rows
-        first = 4 * cache_rows + (lax.axis_index('cp') // 2) * crows
-        cos_t, sin_t = rope_tables(first + jnp.arange(crows), head_dim)
-        bias = jnp.stack([b_q1, b_k1, b_q2, b_k2]).astype(F32)
+        cos_t, sin_t = rope_tables(4 * cache_rows + np.arange(2 * crows), head_dim)
+        bias = [v.reshape(heads, head_dim) for v in (b_q1, b_k1, b_q2, b_k2)]
 
         def flat(c):
             return c.reshape(cache_rows, d_model)
@@ -387,35 +593,33 @@
         out = pl.pallas_call(
             functools.partial(body, (d_model, ff, rows, cache_rows)),
             out_shape=[row_out] * 6,
-            in_specs=[vmem_spec] * 3 + [any_spec] * 16,
+            in_specs=[vmem_spec] * 6 + [any_spec] * 16,
             out_specs=[any_spec] * 6,
             scratch_shapes=[
                 pltpu.VMEM((SLOTS, d_model, TILE), BF16),
-                pltpu.VMEM((crows, d_model), BF16),
-                pltpu.VMEM((crows, d_model), BF16),
-                pltpu.VMEM((crows, d_model), BF16),
-                pltpu.VMEM((crows, d_model), BF16),
+                pltpu.VMEM((2 * crows, d_model), BF16),
+                pltpu.VMEM((2 * crows, d_model), BF16),
                 pltpu.VMEM((crows, ff), BF16),
-                pltpu.VMEM((blocks, 2 * crows, TILE), BF16),
-                pltpu.VMEM((blocks, crows, TILE), BF16),
-                pltpu.VMEM((blocks, crows, TILE), BF16),
+                pltpu.VMEM((2 * blocks, 2 * crows, TILE), BF16),
                 pltpu.VMEM((2 * cache_rows, half), BF16),
                 pltpu.VMEM((2 * cache_rows, half), BF16),
                 pltpu.VMEM((blocks, crows, TILE), F32),
                 pltpu.VMEM((blocks, crows, TILE), F32),
                 pltpu.VMEM((blocks, crows, TILE), F32),
                 pltpu.VMEM((crows, d_model), BF16),
-                pltpu.VMEM((blocks, crows, TILE), BF16),
+                pltpu.VMEM((2 * crows, TILE // 2), BF16),
                 pltpu.VMEM((blocks, crows, HEAD), F32),
                 pltpu.VMEM((blocks, 8, HEAD), F32),
                 pltpu.VMEM((blocks, 8, HEAD), F32),
-                dma((SLOTS,)), dma((3,)), dma((6,)),
+                pltpu.VMEM((4, heads, head_dim), F32),
+                dma((SLOTS,)), dma((3,)), dma((6,)), dma((8,)), dma((8,)),
                 dma((blocks,)), dma((blocks,)), dma((blocks,)), dma((blocks,)), dma((blocks,)), dma((blocks,)),
                 dma((5,)), dma((5,)), dma((6,)), dma((2,)),
+                dma((blocks,)), dma((blocks,)), dma((8,)), dma((8,)),
             ],
             compiler_params=pltpu.CompilerParams(
                 collective_id=0, has_side_effects=True, vmem_limit_bytes=67043328),
-        )(cos_t, sin_t, bias, x_in, flat(cache_k1), flat(cache_v1), flat(cache_k2), flat(cache_v2),
+        )(cos_t, sin_t, *bias, x_in, flat(cache_k1), flat(cache_v1), flat(cache_k2), flat(cache_v2),
           w_q1, w_k1, w_v1, w_o1, w_gate, w_up, w_down, w_q2, w_k2, w_v2, w_o2)
         g, y2, k1, v1, k2, v2 = out
 

time: 204 us -> 189 us (0.926)
  Pallas kernels: 181 us -> 170 us
  local copies, waits for them, and re-layouts: 20.4 us -> 17.6 us
    pallas_call x1, Pallas kernels: 181 us -> 170 us  [forward(): pl.pallas_call(functools.partial(body, (d_model, ff, rows, cache_rows)),...]
    another operation x4 -> x0, local copies, waits for them, and re-layouts: 2.87 us -> none  [forward(): bias = jnp.stack([b_q1, b_k1, b_q2, b_k2]).astype(F32)]
where the time goes in v2:
time: 189 us
  Pallas kernels  170 us (90%)
  local copies, waits for them, and re-layouts  17.6 us (9%)
    pallas_call x1, Pallas kernels, forward(): pl.pallas_call(functools.partial(body, (d_model, ff, rows, cache_rows)),...  170 us
    reshape x2, local copies, waits for them, and re-layouts, flat(): return c.reshape(cache_rows, d_model)  9.71 us
    unnamed x18, local copies, waits for them, and re-layouts  7.85 us

profile of v2, /device:TPU:0, one launch (start us, length us, event | category | flops | bytes accessed | tf_op | source)
XLA Modules:
  0.0 188.6 jit_solution(9809301253193868994)
XLA Ops:
  0.6 0.0 copy-start
  0.6 0.0 copy-start.1
  0.7 6.2 %copy_bitcast_fusion.2 = (bf16[256,5120]{1,0:T(8,128)(2,1)}, bf16[256,5120]{1,0:T(8,128)(2,1)}) fusion(bf16[32,8,40,128]{3,2,1,0:T(8,128)(2,1)} %bitcast.24, bf16[32,8,40,128]{3,2,1,0:T(8,128)(2,1)} %bitcast.25), kind=kLoop, calls=%fused_computation.2 | loop fusion | bytes 10485760 | tf_op jit(solution)/shard_map/reshape | solution.py:587
  6.8 0.0 copy-done
  6.8 0.0 copy-done.1
  6.8 3.5 %copy_bitcast_fusion = (bf16[256,5120]{1,0:T(8,128)(2,1)}, bf16[256,5120]{1,0:T(8,128)(2,1)}) fusion(bf16[32,8,40,128]{3,2,1,0:T(8,128)(2,1)S(1)} %bitcast.26, bf16[32,8,40,128]{3,2,1,0:T(8,128)(2,1)S(1)} %bitcast.27), kind=kLoop, calls=%fused_computation | loop fusion | bytes 10485760 | tf_op jit(solution)/shard_map/reshape | solution.py:587
  10.4 170.4 %shard_map.253 = (bf16[64,5120]{1,0:T(8,128)(2,1)}, bf16[64,5120]{1,0:T(8,128)(2,1)}, bf16[64,5120]{1,0:T(8,128)(2,1)}, bf16[64,5120]{1,0:T(8,128)(2,1)}, bf16[6...) custom-call(f32[256,128]{1,0:T(8,128)} %constant.4.clone.cos_ref, f32[256,128]{1,0:T(8,128)} %constant.5.clone.sin_ref, ...), custom_call_target="tpu_custom_call" | custom-call | tf_op jit(solution)/shard_map/pallas_call | solution.py:593
  180.8 0.0 copy-start.5
  180.8 0.0 copy-start.4
  180.8 0.0 copy-start.3
  180.8 2.2 %copy.32 = bf16[8,8,40,128]{3,2,1,0:T(8,128)(2,1)} copy(bf16[8,8,40,128]{3,1,2,0:T(8,128)(2,1)} %bitcast.35) | data formatting | bytes 1310720
  183.0 0.0 copy-start.2
  183.0 2.1 %copy.33 = bf16[8,8,40,128]{3,2,1,0:T(8,128)(2,1)} copy(bf16[8,8,40,128]{3,1,2,0:T(8,128)(2,1)} %bitcast.34) | data formatting | bytes 1310720
  185.1 0.0 copy-done.5
  185.1 0.9 copy.34
  186.0 0.0 copy-done.4
  186.0 0.9 copy.35
  187.0 0.0 copy-done.3
  187.0 0.8 copy.42
  187.8 0.0 copy-done.2
  187.8 0.8 copy.43
Async XLA Ops:
  0.6 6.2 %copy-start = (bf16[256,40,128]{2,1,0:T(8,128)(2,1)S(1)}, bf16[256,40,128]{2,1,0:T(8,128)(2,1)}, u32[]{:S(2)}) copy-start(bf16[256,40,128]{2,1,0:T(8,128)(2,1)} %param.35) | copy-start | bytes 7864324
  0.6 6.2 %copy-start.1 = (bf16[256,40,128]{2,1,0:T(8,128)(2,1)S(1)}, bf16[256,40,128]{2,1,0:T(8,128)(2,1)}, u32[]{:S(2)}) copy-start(bf16[256,40,128]{2,1,0:T(8,128)(2,1)} %param.34) | copy-start | bytes 7864324
  180.8 4.3 %copy-start.5 = (bf16[64,5120]{1,0:T(8,128)(2,1)S(1)}, bf16[64,5120]{1,0:T(8,128)(2,1)}, u32[]{:S(2)}) copy-start(bf16[64,5120]{1,0:T(8,128)(2,1)} %get-tuple-element.16) | copy-start | bytes 1966084
  180.8 5.2 %copy-start.4 = (bf16[64,5120]{1,0:T(8,128)(2,1)S(1)}, bf16[64,5120]{1,0:T(8,128)(2,1)}, u32[]{:S(2)}) copy-start(bf16[64,5120]{1,0:T(8,128)(2,1)} %get-tuple-element.17) | copy-start | bytes 1966084
  180.8 6.2 %copy-start.3 = (bf16[64,5120]{1,0:T(8,128)(2,1)S(1)}, bf16[64,5120]{1,0:T(8,128)(2,1)}, u32[]{:S(2)}) copy-start(bf16[64,5120]{1,0:T(8,128)(2,1)} %get-tuple-element.28) | copy-start | bytes 1966084
  183.0 4.8 %copy-start.2 = (bf16[64,5120]{1,0:T(8,128)(2,1)S(1)}, bf16[64,5120]{1,0:T(8,128)(2,1)}, u32[]{:S(2)}) copy-start(bf16[64,5120]{1,0:T(8,128)(2,1)} %get-tuple-element.29) | copy-start | bytes 1966084

commit v3 on v2

--- a/solution.py
+++ b/solution.py
@@ -1,4 +1,5 @@
 import functools
+import math
 
 import jax
 import jax.numpy as jnp
@@ -154,7 +155,7 @@
         return pltpu.make_async_remote_copy(src_ref=src, dst_ref=dst, send_sem=send, recv_sem=recv,
                                             device_id={"cp": who}, device_id_type=MESH)
 
-    for s in range(SLOTS):
+    for s in range(2):
         start_tile(s, s, s + 1)
 
     barrier = pltpu.get_barrier_semaphore()
@@ -179,6 +180,8 @@
     cache1 = cache_copies(ck1, cv1)
     for c in cache1:
         c.start()
+    for s in range(2, SLOTS):
+        start_tile(s, s, s + 1)
     for i, ref in enumerate((bq1, bk1, bq2, bk2)):
         bias32[i] = ref[...].astype(F32)
     x_loc.wait()
@@ -205,7 +208,7 @@
     row_i = lax.broadcasted_iota(jnp.int32, (2 * crows, crows), 0)
     col_i = lax.broadcasted_iota(jnp.int32, (2 * crows, crows), 1)
     far_lim = jnp.where(chip == 0, crows, -1)
-    scale = HEAD ** -0.5
+    scale = HEAD ** -0.5 * math.log2(math.e)
 
     def attend(b):
         lane = lax.broadcasted_iota(jnp.int32, (2 * crows, HEAD), 1)
@@ -216,12 +219,12 @@
             at = pl.ds(i * HEAD, HEAD)
             cat = pl.ds(pl.multiple_of(b * TILE + i * HEAD, 128), HEAD)
             q = pre[b, :, at]
-            s_old = lax.dot_general(q, kc[:, cat], dims_t, preferred_element_type=F32) * scale
-            s_new = lax.dot_general(q, pre[blocks + b, pl.ds(0, crows), at], dims_t, preferred_element_type=F32) * scale
+            s_old = lax.dot_general(q, kc[:, cat], dims_t, preferred_element_type=F32)
+            s_new = lax.dot_general(q, pre[blocks + b, pl.ds(0, crows), at], dims_t, preferred_element_type=F32)
             s_new = jnp.where(visible, s_new, -jnp.inf)
             peak = jnp.maximum(jnp.max(s_old, axis=1, keepdims=True), jnp.max(s_new, axis=1, keepdims=True))
-            p_old = jnp.exp(s_old - peak)
-            p_new = jnp.exp(s_new - peak)
+            p_old = jnp.exp2((s_old - peak) * scale)
+            p_new = jnp.exp2((s_new - peak) * scale)
             total_p = jnp.sum(p_old, axis=1, keepdims=True) + jnp.sum(p_new, axis=1, keepdims=True)
             acc = jnp.dot(p_old.astype(BF16), vc[:, cat], preferred_element_type=F32)
             acc = acc + jnp.dot(p_new.astype(BF16), pre[blocks + b, pl.ds(crows, crows), at], preferred_element_type=F32)
@@ -299,7 +302,7 @@
                 m_a, l_a = near[:, 2 * i:2 * i + 1], near[:, 2 * i + 1:2 * i + 2]
                 m_b, l_b = far[:, 2 * i:2 * i + 1], far[:, 2 * i + 1:2 * i + 2]
                 peak = jnp.maximum(m_a, m_b)
-                w_a, w_b = jnp.exp(m_a - peak), jnp.exp(m_b - peak)
+                w_a, w_b = jnp.exp2((m_a - peak) * scale), jnp.exp2((m_b - peak) * scale)
                 norm_l = 1.0 / (l_a * w_a + l_b * w_b)
                 o = o_loc[b, :, at] * (w_a * norm_l) + o_recv[b, :, at] * (w_b * norm_l)
                 obuf[:, pl.ds(pl.multiple_of(core * half + b * TILE + i * HEAD, 128), HEAD)] = o.astype(BF16)
@@ -332,18 +335,29 @@
 
     attention(xin, base1, 0, cache1, k1_out, v1_out)
 
-    def cache2_copy(kv, kind):
+    PIECE = TILE // 2
+
+    def cache2_copy(kv, kind, b=None):
         src, dst = ((ck2, kc), (cv2, vc))[kv]
         who, to_core, to_chip = ((None, core, chip), (partner, 1 - core, chip), (peer, core, 1 - chip),
                                  (diag, 1 - core, 1 - chip))[kind]
+        off, width, sem = (0, quart, 0) if b is None else (b * PIECE, PIECE, 1 + b)
         side = 0 if kind < 2 else quart
-        from_at = pl.ds(pl.multiple_of(to_core * half + to_chip * quart, 128), quart)
-        to = dst.at[pl.ds(pl.multiple_of(core * cache_rows, 16), cache_rows), pl.ds(side, quart)]
+        from_at = pl.ds(pl.multiple_of(to_core * half + to_chip * quart + off, 128), width)
+        to = dst.at[pl.ds(pl.multiple_of(core * cache_rows, 16), cache_rows), pl.ds(pl.multiple_of(side + off, 128), width)]
+        i = 4 * kv + kind
         if kind == 0:
-            return pltpu.make_async_copy(src.at[:, from_at], to, c2send.at[4 * kv])
-        return remote(src.at[:, from_at], to, c2send.at[4 * kv + kind], c2recv.at[4 * kv + kind], who)
-
-    for kind in (2, 3, 1, 0):
+            return pltpu.make_async_copy(src.at[:, from_at], to, c2send.at[i])
+        return remote(src.at[:, from_at], to, c2send.at[i], c2recv.at[i, sem], who)
+
+    def far_cache(b):
+        for kv in range(2):
+            for kind in (2, 3):
+                cache2_copy(kv, kind, b).start()
+
+    for b in range(3):
+        far_cache(b)
+    for kind in (1, 0):
         for kv in range(2):
             cache2_copy(kv, kind).start()
 
@@ -371,6 +385,10 @@
         at = pl.ds(pl.multiple_of(core * ffh + n * (TILE // 2), 128), TILE // 2)
         ebuf[:, at] = (jax.nn.silu(gate) * up).astype(BF16)
         remote(ebuf.at[:, at], ebuf.at[:, at], dsend.at[2], drecv.at[2], partner).start()
+
+        @pl.when(n == ffn // 2)
+        def _():
+            far_cache(3)
 
     both_wait(ebuf, 2, ffh, pl.multiple_of(core * ffh, 128), pl.multiple_of((1 - core) * ffh, 128))
 
@@ -398,9 +416,12 @@
         remote(mine, theirs, dsend.at[sem], drecv.at[sem], partner).wait_send()
         remote(mine, theirs, dsend.at[sem], drecv.at[sem], partner).wait_recv()
 
+    far_cache(4)
     g_wait(chip_rows, 3)
-    g_copy = pltpu.make_async_copy(gbuf.at[pl.ds(pl.multiple_of(chip_rows + my_rows, 16), rows), :], g_out, gsem.at[0])
-    g_copy.start()
+    g_rows = pl.ds(pl.multiple_of(chip_rows + my_rows, 16), rows)
+    g_copies = [pltpu.make_async_copy(gbuf.at[g_rows, pl.ds(j * TILE, TILE)], g_out.at[j], gsem.at[0]) for j in range(2 * blocks)]
+    for c in g_copies:
+        c.start()
     norm(gbuf, nbuf, chip_rows, crows)
 
     @pl.loop(0, blocks)
@@ -429,13 +450,13 @@
             far = pl.ds(pl.multiple_of(quart + b * PAIR + i * HEAD, 128), HEAD)
             v_at = pl.ds(pl.multiple_of(lax.rem(b, 2) * PAIR + i * HEAD, 128), HEAD)
             q = pre[t, :, pl.ds(i * HEAD, HEAD)]
-            s_a = lax.dot_general(q, kc[:, near], dims_t, preferred_element_type=F32) * scale
-            s_b = lax.dot_general(q, kc[:, far], dims_t, preferred_element_type=F32) * scale
-            s_n = lax.dot_general(q, pre[t, :, pl.ds(PAIR + i * HEAD, HEAD)], dims_t, preferred_element_type=F32) * scale
+            s_a = lax.dot_general(q, kc[:, near], dims_t, preferred_element_type=F32)
+            s_b = lax.dot_general(q, kc[:, far], dims_t, preferred_element_type=F32)
+            s_n = lax.dot_general(q, pre[t, :, pl.ds(PAIR + i * HEAD, HEAD)], dims_t, preferred_element_type=F32)
             s_n = jnp.where(visible, s_n, -jnp.inf)
             peak = jnp.maximum(jnp.maximum(jnp.max(s_a, axis=1, keepdims=True), jnp.max(s_b, axis=1, keepdims=True)),
                                jnp.max(s_n, axis=1, keepdims=True))
-            p_a, p_b, p_n = jnp.exp(s_a - peak), jnp.exp(s_b - peak), jnp.exp(s_n - peak)
+            p_a, p_b, p_n = (jnp.exp2((s - peak) * scale) for s in (s_a, s_b, s_n))
             total_p = (jnp.sum(p_a, axis=1, keepdims=True) + jnp.sum(p_b, axis=1, keepdims=True)
                        + jnp.sum(p_n, axis=1, keepdims=True))
             acc = jnp.dot(p_a.astype(BF16), vc[:, near], preferred_element_type=F32)
@@ -498,9 +519,12 @@
             @pl.when(b == 0)
             def _():
                 for kv in range(2):
-                    for kind in range(4):
+                    for kind in range(2):
                         cache2_copy(kv, kind).wait()
 
+            for kv in range(2):
+                for kind in (2, 3):
+                    cache2_copy(kv, kind, b).wait_recv()
             attend2(b)
             obuf[:, pl.ds(pl.multiple_of(chip * quart + b * PAIR, 128), PAIR)] = opair[pl.ds(chip_rows, crows), :]
             obuf[:, pl.ds(pl.multiple_of(half + b * PAIR, 128), PAIR)] = opair[pl.ds(far_rows, crows), :]
@@ -545,8 +569,9 @@
             at = pl.ds(i * rows, rows)
             ybuf[:, pl.ds(pl.multiple_of(b * 2 * TILE + i * TILE, 128), TILE)] = (o_loc[b, at, :] + o_recv[b, at, :]).astype(BF16)
 
-    y_copy_out = pltpu.make_async_copy(ybuf, y_out, gsem.at[1])
-    y_copy_out.start()
+    y_copies = [pltpu.make_async_copy(ybuf.at[:, pl.ds(j * TILE, TILE)], y_out.at[j], gsem.at[1]) for j in range(2 * blocks)]
+    for c in y_copies:
+        c.start()
 
     @pl.loop(0, blocks)
     def _(b):
@@ -560,8 +585,10 @@
         for kind, who in ((1, partner), (2, peer), (3, diag)):
             remote(ref, ref, a2send.at[4 * kv + kind], a2recv.at[4 * kv + kind], who).wait_send()
             remote(ref, ref, a2send.at[4 * kv + kind], a2recv.at[4 * kv + kind], who).wait_recv()
-    y_copy_out.wait()
-    g_copy.wait()
+        for kind in (2, 3):
+            cache2_copy(kv, kind).wait_send()
+    for ref, sem in ((y_out, 1), (g_out, 0)):
+        pltpu.make_async_copy(ref, ref, gsem.at[sem]).wait()
 
 
 def solution(mesh):
@@ -588,11 +615,12 @@
 
         any_spec = pl.BlockSpec(memory_space=pl.ANY)
         vmem_spec = pl.BlockSpec(memory_space=pltpu.VMEM)
+        blocked = jax.ShapeDtypeStruct((2 * blocks, rows, TILE), BF16)
         row_out = jax.ShapeDtypeStruct((rows, d_model), BF16)
         dma = pltpu.SemaphoreType.DMA
         out = pl.pallas_call(
             functools.partial(body, (d_model, ff, rows, cache_rows)),
-            out_shape=[row_out] * 6,
+            out_shape=[blocked] * 2 + [row_out] * 4,
             in_specs=[vmem_spec] * 6 + [any_spec] * 16,
             out_specs=[any_spec] * 6,
             scratch_shapes=[
@@ -612,7 +640,7 @@
                 pltpu.VMEM((blocks, 8, HEAD), F32),
                 pltpu.VMEM((blocks, 8, HEAD), F32),
                 pltpu.VMEM((4, heads, head_dim), F32),
-                dma((SLOTS,)), dma((3,)), dma((6,)), dma((8,)), dma((8,)),
+                dma((SLOTS,)), dma((3,)), dma((6,)), dma((8,)), dma((8, 6)),
                 dma((blocks,)), dma((blocks,)), dma((blocks,)), dma((blocks,)), dma((blocks,)), dma((blocks,)),
                 dma((5,)), dma((5,)), dma((6,)), dma((2,)),
                 dma((blocks,)), dma((blocks,)), dma((8,)), dma((8,)),
@@ -626,6 +654,9 @@
         def heads_of(a):
             return a.reshape(rows, heads, head_dim)
 
-        return g, y2, heads_of(k1), heads_of(v1), heads_of(k2), heads_of(v2)
+        def unblock(a):
+            return a.transpose(1, 0, 2).reshape(rows, d_model)
+
+        return unblock(g), unblock(y2), heads_of(k1), heads_of(v1), heads_of(k2), heads_of(v2)
 
     return jax.shard_map(forward, mesh=mesh, in_specs=in_specs, out_specs=out_specs, check_vma=False)

time: 189 us -> 175 us (0.926)
  Pallas kernels: 170 us -> 157 us
    pallas_call x1, Pallas kernels: 170 us -> 157 us  [forward(): pl.pallas_call(functools.partial(body, (d_model, ff, rows, cache_rows)),...]
    reshape x0 -> x2, local copies, waits for them, and re-layouts: none -> 4.18 us  [unblock(): return a.transpose(1, 0, 2).reshape(rows, d_model)]
    unnamed x18 -> x16, local copies, waits for them, and re-layouts: 7.85 us -> 3.8 us
where the time goes in v3:
time: 175 us
  Pallas kernels  157 us (90%)
  local copies, waits for them, and re-layouts  17.7 us (10%)
    pallas_call x1, Pallas kernels, forward(): pl.pallas_call(functools.partial(body, (d_model, ff, rows, cache_rows)),...  157 us
    reshape x2, local copies, waits for them, and re-layouts, flat(): return c.reshape(cache_rows, d_model)  9.71 us
    reshape x2, local copies, waits for them, and re-layouts, unblock(): return a.transpose(1, 0, 2).reshape(rows, d_model)  4.18 us
    unnamed x16, local copies, waits for them, and re-layouts  3.8 us

profile of v3, /device:TPU:0, one launch (start us, length us, event | category | flops | bytes accessed | tf_op | source)
XLA Modules:
  0.0 175.3 jit_solution(8847495021870255254)
XLA Ops:
  0.6 0.0 copy-start
  0.6 0.0 copy-start.1
  0.7 6.2 %copy_bitcast_fusion.2 = (bf16[256,5120]{1,0:T(8,128)(2,1)}, bf16[256,5120]{1,0:T(8,128)(2,1)}) fusion(bf16[32,8,40,128]{3,2,1,0:T(8,128)(2,1)} %bitcast.30, bf16[32,8,40,128]{3,2,1,0:T(8,128)(2,1)} %bitcast.31), kind=kLoop, calls=%fused_computation.2 | loop fusion | bytes 10485760 | tf_op jit(solution)/shard_map/reshape | solution.py:614
  6.8 0.0 copy-done
  6.8 0.0 copy-done.1
  6.8 3.5 %copy_bitcast_fusion = (bf16[256,5120]{1,0:T(8,128)(2,1)}, bf16[256,5120]{1,0:T(8,128)(2,1)}) fusion(bf16[32,8,40,128]{3,2,1,0:T(8,128)(2,1)S(1)} %bitcast.32, bf16[32,8,40,128]{3,2,1,0:T(8,128)(2,1)S(1)} %bitcast.33), kind=kLoop, calls=%fused_computation | loop fusion | bytes 10485760 | tf_op jit(solution)/shard_map/reshape | solution.py:614
  10.4 156.9 %shard_map.253 = (bf16[10,64,512]{2,1,0:T(8,128)(2,1)}, bf16[10,64,512]{2,1,0:T(8,128)(2,1)}, bf16[64,5120]{1,0:T(8,128)(2,1)}, bf16[64,5120]{1,0:T(8,128)(2,1)}...) custom-call(f32[256,128]{1,0:T(8,128)} %constant.4.clone.cos_ref, f32[256,128]{1,0:T(8,128)} %constant.5.clone.sin_ref, ...), custom_call_target="tpu_custom_call" | custom-call | tf_op jit(solution)/shard_map/pallas_call | solution.py:621
  167.3 0.0 copy-start.5
  167.3 0.0 copy-start.4
  167.3 0.0 copy-start.3
  167.3 2.1 %copy.30 = bf16[10,8,8,512]{3,2,0,1:T(8,128)(2,1)} copy(bf16[10,8,8,512]{3,2,1,0:T(8,128)(2,1)} %bitcast.45) | data formatting | bytes 1310720 | tf_op jit(solution)/shard_map/reshape | solution.py:658
  169.4 0.0 copy-start.2
  169.4 2.1 %copy.31 = bf16[10,8,8,512]{3,2,0,1:T(8,128)(2,1)} copy(bf16[10,8,8,512]{3,2,1,0:T(8,128)(2,1)} %bitcast.44) | data formatting | bytes 1310720 | tf_op jit(solution)/shard_map/reshape | solution.py:658
  171.5 0.0 copy-done.5
  171.5 0.9 copy.36
  172.4 0.0 copy-done.4
  172.5 0.9 copy.37
  173.4 0.0 copy-done.3
  173.4 0.9 copy.38
  174.3 0.0 copy-done.2
  174.3 0.9 copy.39
Async XLA Ops:
  0.6 6.2 %copy-start = (bf16[256,40,128]{2,1,0:T(8,128)(2,1)S(1)}, bf16[256,40,128]{2,1,0:T(8,128)(2,1)}, u32[]{:S(2)}) copy-start(bf16[256,40,128]{2,1,0:T(8,128)(2,1)} %param.35) | copy-start | bytes 7864324
  0.6 6.2 %copy-start.1 = (bf16[256,40,128]{2,1,0:T(8,128)(2,1)S(1)}, bf16[256,40,128]{2,1,0:T(8,128)(2,1)}, u32[]{:S(2)}) copy-start(bf16[256,40,128]{2,1,0:T(8,128)(2,1)} %param.34) | copy-start | bytes 7864324
  167.3 4.2 %copy-start.5 = (bf16[64,5120]{1,0:T(8,128)(2,1)S(1)}, bf16[64,5120]{1,0:T(8,128)(2,1)}, u32[]{:S(2)}) copy-start(bf16[64,5120]{1,0:T(8,128)(2,1)} %get-tuple-element.14) | copy-start | bytes 1966084
  167.3 5.1 %copy-start.4 = (bf16[64,5120]{1,0:T(8,128)(2,1)S(1)}, bf16[64,5120]{1,0:T(8,128)(2,1)}, u32[]{:S(2)}) copy-start(bf16[64,5120]{1,0:T(8,128)(2,1)} %get-tuple-element.15) | copy-start | bytes 1966084
  167.3 6.1 %copy-start.3 = (bf16[64,5120]{1,0:T(8,128)(2,1)S(1)}, bf16[64,5120]{1,0:T(8,128)(2,1)}, u32[]{:S(2)}) copy-start(bf16[64,5120]{1,0:T(8,128)(2,1)} %get-tuple-element.16) | copy-start | bytes 1966084
  169.4 4.9 %copy-start.2 = (bf16[64,5120]{1,0:T(8,128)(2,1)S(1)}, bf16[64,5120]{1,0:T(8,128)(2,1)}, u32[]{:S(2)}) copy-start(bf16[64,5120]{1,0:T(8,128)(2,1)} %get-tuple-element.17) | copy-start | bytes 1966084

commit v4 on v3

--- a/solution.py
+++ b/solution.py
@@ -34,11 +34,13 @@
          wring, nbuf, gbuf, ebuf, pre, kc, vc, o_loc, o_send, o_recv, obuf, opair,
          st_loc, st_send, st_recv, bias32,
          wsem, xsem, csem, c2send, c2recv, qsend, qrecv, osend, orecv, ssend, srecv, dsend, drecv, asem, gsem,
-         gxs, gxr, a2send, a2recv):
+         gxs, gxr, a2send, a2recv, hys, hyr, esem, yfree):
     d_model, ff, rows, cache_rows = dims
     half = d_model // 2
     ffh = ff // 2
     ffc = ff // 3
+    third = ffc // 2
+    part = third // (TILE // 2)
     blocks = half // TILE
     ffn = ffh // (TILE // 2)
     crows = 2 * rows
@@ -50,6 +52,8 @@
     partner = me + 1 - 2 * core
     peer = lax.rem(me + 2, 4)
     diag = 3 - me
+    dp = lax.axis_index("dp")
+    side_y = 1 - dp
     chip_rows = pl.multiple_of(chip * crows, 16)
     xin = hbuf = gbuf.at[pl.ds(pl.multiple_of(chip * crows, 16), crows), :]
     far_rows = pl.multiple_of((1 - chip) * crows, 16)
@@ -64,22 +68,29 @@
     attn_tiles = 4 * blocks
     base1 = 0
     base_up = attn_tiles
-    base_down = base_up + ffn
+    base_down = base_up + 2 * part
     base2 = base_down + 3 * blocks
     qkv2 = 8
 
     def start_full(w, b, slot):
         pltpu.make_async_copy(w.at[:, pl.ds(col(b), TILE)], wring.at[slot], wsem.at[slot]).start()
 
-    def start_mlp(n, slot):
-        at = pl.ds(pl.multiple_of(core * ffh + n * (TILE // 2), 128), TILE // 2)
+    def mlp_cols(tile):
+        return pl.ds(pl.multiple_of(core * ffh + tile * (TILE // 2), 128), TILE // 2)
+
+    def shared_tile(n):
+        return part + dp * part + n
+
+    def start_mlp(tile, slot):
+        at = mlp_cols(tile)
         pltpu.make_async_copy(w_gate.at[:, at], wring.at[slot, :, pl.ds(0, TILE // 2)], wsem.at[slot]).start()
         pltpu.make_async_copy(w_up.at[:, at], wring.at[slot, :, pl.ds(TILE // 2, TILE // 2)], wsem.at[slot]).start()
 
-    def start_down(i, slot):
-        pltpu.make_async_copy(
-            w_down.at[pl.ds(pl.multiple_of(lax.rem(i, 3) * ffc, 16), ffc), pl.ds(col(i // 3), TILE)],
-            wring.at[slot, pl.ds(0, ffc), :], wsem.at[slot]).start()
+    def start_down(b, chunk, slot):
+        for i in range(2):
+            pltpu.make_async_copy(
+                w_down.at[pl.ds(pl.multiple_of(i * ffh + chunk * third, 16), third), pl.ds(col(b), TILE)],
+                wring.at[slot, pl.ds(i * third, third), :], wsem.at[slot]).start()
 
     loop_end = 3 * (blocks - 1) + 1
 
@@ -120,8 +131,10 @@
                 wring.at[slot, pl.ds(i * half, half), :], wsem.at[slot]).start()
 
     segments = attn_segments(base1, wq1, wk1, wv1, wo1) + [
-        (base_up, base_down, start_mlp, None),
-        (base_down, base2, start_down, None),
+        (base_up, base_up + part, start_mlp, None),
+        (base_up + part, base_down, lambda r, slot: start_mlp(shared_tile(r), slot), None),
+        (base_down, base_down + blocks, lambda r, slot: start_down(r, 0, slot), None),
+        (base_down + blocks, base2, lambda r, slot: start_down(r // 2, 1 + r % 2 if isinstance(r, int) else 1 + lax.rem(r, 2), slot), None),
         (base2, base2 + qkv2, start_v2, 0),
         (base2, base2 + qkv2, start_qk2, 1),
         (base2, base2 + qkv2, start_qk2, 2),
@@ -155,13 +168,18 @@
         return pltpu.make_async_remote_copy(src_ref=src, dst_ref=dst, send_sem=send, recv_sem=recv,
                                             device_id={"cp": who}, device_id_type=MESH)
 
+    def remote_y(src, dst, send, recv):
+        return pltpu.make_async_remote_copy(src_ref=src, dst_ref=dst, send_sem=send, recv_sem=recv,
+                                            device_id={"dp": side_y}, device_id_type=MESH)
+
     for s in range(2):
         start_tile(s, s, s + 1)
 
     barrier = pltpu.get_barrier_semaphore()
     for who in (partner, peer, diag):
         pl.semaphore_signal(barrier, inc=1, device_id={"cp": who}, device_id_type=MESH)
-    pl.semaphore_wait(barrier, 3)
+    pl.semaphore_signal(barrier, inc=1, device_id={"dp": side_y}, device_id_type=MESH)
+    pl.semaphore_wait(barrier, 4)
 
     x_loc = pltpu.make_async_copy(x_hbm, xin.at[pl.ds(my_rows, rows)], xsem.at[0])
     x_rem = remote(x_hbm, xin.at[pl.ds(my_rows, rows)], xsem.at[1], xsem.at[2], partner)
@@ -334,6 +352,7 @@
         remote(mine, theirs, dsend.at[sem], drecv.at[sem], partner).wait_recv()
 
     attention(xin, base1, 0, cache1, k1_out, v1_out)
+    pl.semaphore_signal(yfree, inc=1, device_id={"dp": side_y}, device_id_type=MESH)
 
     PIECE = TILE // 2
 
@@ -361,6 +380,11 @@
         for kv in range(2):
             cache2_copy(kv, kind).start()
 
+    pl.semaphore_wait(yfree, 1)
+
+    def h_copy(b):
+        return remote_y(hbuf.at[:, pl.ds(col(b), TILE)], pre.at[core * blocks + b, pl.ds(0, crows), :], hys.at[b], hyr.at[b])
+
     @pl.loop(0, blocks)
     def _(b):
         s = base1 + 3 * blocks + b
@@ -369,28 +393,99 @@
         start_tile(s + SLOTS, base1 + 3 * blocks + SLOTS, base_up + SLOTS)
         at = pl.ds(col(b), TILE)
         hbuf[:, at] = (xin[:, at].astype(F32) + y.astype(F32)).astype(BF16)
+        h_copy(b).start()
         remote(hbuf.at[:, at], hbuf.at[:, at], dsend.at[1], drecv.at[1], partner).start()
 
     both_wait(hbuf, 1, half, my_cols, other_cols)
     norm(hbuf, nbuf, 0, crows)
 
-    @pl.loop(0, ffn)
+    def glu(both):
+        gate = both[:, :TILE // 2].astype(BF16).astype(F32)
+        up = both[:, TILE // 2:].astype(BF16).astype(F32)
+        return (jax.nn.silu(gate) * up).astype(BF16)
+
+    @pl.loop(0, part)
     def _(n):
         s = base_up + n
         slot = wait_tile(s)
         both = jnp.dot(nbuf[pl.ds(0, crows), :], wring[slot], preferred_element_type=F32)
-        start_tile(s + SLOTS, base_up + SLOTS, base_down + SLOTS)
-        gate = both[:, :TILE // 2].astype(BF16).astype(F32)
-        up = both[:, TILE // 2:].astype(BF16).astype(F32)
-        at = pl.ds(pl.multiple_of(core * ffh + n * (TILE // 2), 128), TILE // 2)
-        ebuf[:, at] = (jax.nn.silu(gate) * up).astype(BF16)
+        start_tile(s + SLOTS, base_up + SLOTS, base_up + part + SLOTS)
+        at = mlp_cols(n)
+        ebuf[:, at] = glu(both)
         remote(ebuf.at[:, at], ebuf.at[:, at], dsend.at[2], drecv.at[2], partner).start()
 
-        @pl.when(n == ffn // 2)
+    far_h = pre.at[pl.ds(core * blocks, blocks), pl.ds(0, crows), :]
+    far_h_other = pre.at[pl.ds((1 - core) * blocks, blocks), pl.ds(0, crows), :]
+
+    @pl.loop(0, blocks)
+    def _(b):
+        h_copy(b).wait_recv()
+        h_copy(b).wait_send()
+
+    remote(far_h, far_h, dsend.at[4], drecv.at[4], partner).start()
+    remote(far_h, far_h, dsend.at[4], drecv.at[4], partner).wait_send()
+    remote(far_h_other, far_h_other, dsend.at[4], drecv.at[4], partner).wait_recv()
+
+    @pl.loop(0, crows // 16)
+    def _(i):
+        at = pl.ds(pl.multiple_of(i * 16, 16), 16)
+        wide = [pre[j, at, :].astype(F32) for j in range(2 * blocks)]
+        square = sum(jnp.sum(w * w, axis=-1, keepdims=True) for w in wide)
+        inv = lax.rsqrt(square / d_model + NORM_EPS)
+        for j in range(2 * blocks):
+            nbuf[pl.ds(pl.multiple_of(crows + i * 16, 16), 16), pl.ds(j * TILE, TILE)] = (wide[j] * inv).astype(BF16)
+
+    def e_return(n):
+        return remote_y(pre.at[n, pl.ds(crows, crows), pl.ds(0, TILE // 2)], ebuf.at[:, mlp_cols(shared_tile(n))],
+                        esem.at[0], esem.at[1])
+
+    @pl.loop(0, part)
+    def _(n):
+        s = base_up + part + n
+        slot = wait_tile(s)
+        both = jnp.dot(nbuf[...], wring[slot], preferred_element_type=F32)
+        start_tile(s + SLOTS, base_up + part + SLOTS, base_down + SLOTS)
+        at = mlp_cols(shared_tile(n))
+        mixed = glu(both)
+        ebuf[:, at] = mixed[:crows]
+        pre[n, pl.ds(crows, crows), pl.ds(0, TILE // 2)] = mixed[crows:]
+        e_return(n).start()
+        remote(ebuf.at[:, at], ebuf.at[:, at], dsend.at[2], drecv.at[2], partner).start()
+
+    def returned(to_core):
+        return ebuf.at[:, pl.ds(pl.multiple_of(to_core * ffh + (1 + side_y) * third, 128), third)]
+
+    def partner_e_wait():
+        some = ebuf.at[:, pl.ds(0, 2 * third)]
+        remote(some, some, dsend.at[2], drecv.at[2], partner).wait_send()
+        remote(some, some, dsend.at[2], drecv.at[2], partner).wait_recv()
+
+    partner_e_wait()
+
+    def down_dot(slot, chunk):
+        out = None
+        for i in range(2):
+            at = pl.ds(pl.multiple_of(i * ffh + chunk * third, 128), third)
+            term = jnp.dot(ebuf[:, at], wring[slot, i * third:(i + 1) * third, :], preferred_element_type=F32)
+            out = term if out is None else out + term
+        return out
+
+    @pl.loop(0, blocks)
+    def _(b):
+        @pl.when(b == blocks - 2)
         def _():
-            far_cache(3)
-
-    both_wait(ebuf, 2, ffh, pl.multiple_of(core * ffh, 128), pl.multiple_of((1 - core) * ffh, 128))
+            e_all = remote_y(returned(core), returned(core), esem.at[0], esem.at[1])
+            e_all.wait_send()
+            e_all.wait_recv()
+            remote(returned(core), returned(core), dsend.at[1], drecv.at[1], partner).start()
+
+        s = base_down + b
+        slot = wait_tile(s, ffc)
+        o_loc[b] = down_dot(slot, 0)
+        start_tile(s + SLOTS, base_down + SLOTS, base_down + blocks + SLOTS)
+
+    remote(returned(core), returned(core), dsend.at[1], drecv.at[1], partner).wait_send()
+    remote(returned(1 - core), returned(1 - core), dsend.at[1], drecv.at[1], partner).wait_recv()
 
     def g_piece(b, first):
         return gbuf.at[pl.ds(first, crows), pl.ds(col(b), TILE)]
@@ -398,14 +493,13 @@
     @pl.loop(0, blocks)
     def _(b):
         at = pl.ds(col(b), TILE)
-        acc = hbuf[:, at].astype(F32)
-        for k in range(3):
-            s = base_down + 3 * b + k
+        down = o_loc[b]
+        for k in range(2):
+            s = base_down + blocks + 2 * b + k
             slot = wait_tile(s, ffc)
-            part = jnp.dot(ebuf[:, k * ffc:(k + 1) * ffc], wring[slot, :ffc, :], preferred_element_type=F32)
-            start_tile(s + SLOTS, base_down + k + SLOTS, base2 - 2 + k + SLOTS)
-            down = part if k == 0 else down + part
-        gbuf[pl.ds(chip_rows, crows), at] = (acc + down).astype(BF16)
+            down = down + down_dot(slot, 1 + k)
+            start_tile(s + SLOTS, base_down + blocks + k + SLOTS, base2 - 1 + k + SLOTS)
+        gbuf[pl.ds(chip_rows, crows), at] = (hbuf[:, at].astype(F32) + down).astype(BF16)
         piece = g_piece(b, chip_rows)
         remote(piece, piece, gxs.at[b], gxr.at[b], peer).start()
         remote(piece, piece, dsend.at[3], drecv.at[3], partner).start()
@@ -416,6 +510,7 @@
         remote(mine, theirs, dsend.at[sem], drecv.at[sem], partner).wait_send()
         remote(mine, theirs, dsend.at[sem], drecv.at[sem], partner).wait_recv()
 
+    far_cache(3)
     far_cache(4)
     g_wait(chip_rows, 3)
     g_rows = pl.ds(pl.multiple_of(chip_rows + my_rows, 16), rows)
@@ -486,7 +581,7 @@
             else:
                 remote(part, dst.at[:, to_at], a2send.at[4 * kv + kind], a2recv.at[4 * kv + kind], who).start()
 
-    early = 2
+    early = 1
 
     @pl.loop(0, qkv2)
     def _(t):
@@ -644,6 +739,7 @@
                 dma((blocks,)), dma((blocks,)), dma((blocks,)), dma((blocks,)), dma((blocks,)), dma((blocks,)),
                 dma((5,)), dma((5,)), dma((6,)), dma((2,)),
                 dma((blocks,)), dma((blocks,)), dma((8,)), dma((8,)),
+                dma((blocks,)), dma((blocks,)), dma((2,)), pltpu.SemaphoreType.REGULAR,
             ],
             compiler_params=pltpu.CompilerParams(
                 collective_id=0, has_side_effects=True, vmem_limit_bytes=67043328),

time: 175 us -> 176 us (level)
  no operation moved by 1% of the time
where the time goes in v4:
time: 176 us
  Pallas kernels  157 us (89%)
  local copies, waits for them, and re-layouts  17.7 us (10%)
    pallas_call x1, Pallas kernels, forward(): pl.pallas_call(functools.partial(body, (d_model, ff, rows, cache_rows)),...  157 us
    reshape x2, local copies, waits for them, and re-layouts, flat(): return c.reshape(cache_rows, d_model)  9.71 us
    reshape x2, local copies, waits for them, and re-layouts, unblock(): return a.transpose(1, 0, 2).reshape(rows, d_model)  4.18 us
    unnamed x16, local copies, waits for them, and re-layouts  3.8 us

profile of v4, /device:TPU:0, one launch (start us, length us, event | category | flops | bytes accessed | tf_op | source)
XLA Modules:
  0.0 175.5 jit_solution(13129502290475458066)
XLA Ops:
  0.6 0.0 copy-start
  0.6 0.0 copy-start.1
  0.7 6.2 %copy_bitcast_fusion.2 = (bf16[256,5120]{1,0:T(8,128)(2,1)}, bf16[256,5120]{1,0:T(8,128)(2,1)}) fusion(bf16[32,8,40,128]{3,2,1,0:T(8,128)(2,1)} %bitcast.30, bf16[32,8,40,128]{3,2,1,0:T(8,128)(2,1)} %bitcast.31), kind=kLoop, calls=%fused_computation.2 | loop fusion | bytes 10485760 | tf_op jit(solution)/shard_map/reshape | solution.py:709
  6.8 0.0 copy-done
  6.8 0.0 copy-done.1
  6.8 3.5 %copy_bitcast_fusion = (bf16[256,5120]{1,0:T(8,128)(2,1)}, bf16[256,5120]{1,0:T(8,128)(2,1)}) fusion(bf16[32,8,40,128]{3,2,1,0:T(8,128)(2,1)S(1)} %bitcast.32, bf16[32,8,40,128]{3,2,1,0:T(8,128)(2,1)S(1)} %bitcast.33), kind=kLoop, calls=%fused_computation | loop fusion | bytes 10485760 | tf_op jit(solution)/shard_map/reshape | solution.py:709
  10.4 157.1 %shard_map.253 = (bf16[10,64,512]{2,1,0:T(8,128)(2,1)}, bf16[10,64,512]{2,1,0:T(8,128)(2,1)}, bf16[64,5120]{1,0:T(8,128)(2,1)}, bf16[64,5120]{1,0:T(8,128)(2,1)}...) custom-call(f32[256,128]{1,0:T(8,128)} %constant.4.clone.cos_ref, f32[256,128]{1,0:T(8,128)} %constant.5.clone.sin_ref, ...), custom_call_target="tpu_custom_call" | custom-call | tf_op jit(solution)/shard_map/pallas_call | solution.py:716
  167.5 0.0 copy-start.5
  167.5 0.0 copy-start.4
  167.5 0.0 copy-start.3
  167.5 2.1 %copy.30 = bf16[10,8,8,512]{3,2,0,1:T(8,128)(2,1)} copy(bf16[10,8,8,512]{3,2,1,0:T(8,128)(2,1)} %bitcast.45) | data formatting | bytes 1310720 | tf_op jit(solution)/shard_map/reshape | solution.py:754
  169.7 0.0 copy-start.2
  169.7 2.1 %copy.31 = bf16[10,8,8,512]{3,2,0,1:T(8,128)(2,1)} copy(bf16[10,8,8,512]{3,2,1,0:T(8,128)(2,1)} %bitcast.44) | data formatting | bytes 1310720 | tf_op jit(solution)/shard_map/reshape | solution.py:754
  171.7 0.0 copy-done.5
  171.7 0.9 copy.36
  172.7 0.0 copy-done.4
  172.7 0.9 copy.37
  173.6 0.0 copy-done.3
  173.6 0.9 copy.38
  174.6 0.0 copy-done.2
  174.6 0.9 copy.39
Async XLA Ops:
  0.6 6.2 %copy-start = (bf16[256,40,128]{2,1,0:T(8,128)(2,1)S(1)}, bf16[256,40,128]{2,1,0:T(8,128)(2,1)}, u32[]{:S(2)}) copy-start(bf16[256,40,128]{2,1,0:T(8,128)(2,1)} %param.35) | copy-start | bytes 7864324
  0.6 6.2 %copy-start.1 = (bf16[256,40,128]{2,1,0:T(8,128)(2,1)S(1)}, bf16[256,40,128]{2,1,0:T(8,128)(2,1)}, u32[]{:S(2)}) copy-start(bf16[256,40,128]{2,1,0:T(8,128)(2,1)} %param.34) | copy-start | bytes 7864324
  167.5 4.2 %copy-start.5 = (bf16[64,5120]{1,0:T(8,128)(2,1)S(1)}, bf16[64,5120]{1,0:T(8,128)(2,1)}, u32[]{:S(2)}) copy-start(bf16[64,5120]{1,0:T(8,128)(2,1)} %get-tuple-element.14) | copy-start | bytes 1966084
  167.5 5.1 %copy-start.4 = (bf16[64,5120]{1,0:T(8,128)(2,1)S(1)}, bf16[64,5120]{1,0:T(8,128)(2,1)}, u32[]{:S(2)}) copy-start(bf16[64,5120]{1,0:T(8,128)(2,1)} %get-tuple-element.15) | copy-start | bytes 1966084
  167.5 6.1 %copy-start.3 = (bf16[64,5120]{1,0:T(8,128)(2,1)S(1)}, bf16[64,5120]{1,0:T(8,128)(2,1)}, u32[]{:S(2)}) copy-start(bf16[64,5120]{1,0:T(8,128)(2,1)} %get-tuple-element.16) | copy-start | bytes 1966084
  169.7 4.9 %copy-start.2 = (bf16[64,5120]{1,0:T(8,128)(2,1)S(1)}, bf16[64,5120]{1,0:T(8,128)(2,1)}, u32[]{:S(2)}) copy-start(bf16[64,5120]{1,0:T(8,128)(2,1)} %get-tuple-element.17) | copy-start | bytes 1966084

commit v5 on v4

--- a/solution.py
+++ b/solution.py
@@ -69,7 +69,8 @@
     base1 = 0
     base_up = attn_tiles
     base_down = base_up + 2 * part
-    base2 = base_down + 3 * blocks
+    base_x = base_down + 3 * blocks
+    base2 = base_x + blocks
     qkv2 = 8
 
     def start_full(w, b, slot):
@@ -124,6 +125,13 @@
         pltpu.make_async_copy(wq2.at[:, at], wring.at[slot, :, pl.ds(0, PAIR)], wsem.at[slot]).start()
         pltpu.make_async_copy(wk2.at[:, at], wring.at[slot, :, pl.ds(PAIR, PAIR)], wsem.at[slot]).start()
 
+    other2 = core * half + (1 - chip) * quart
+
+    def start_kv_other(b, slot):
+        at = pl.ds(pl.multiple_of(other2 + b * PAIR, 128), PAIR)
+        pltpu.make_async_copy(wk2.at[:, at], wring.at[slot, :, pl.ds(0, PAIR)], wsem.at[slot]).start()
+        pltpu.make_async_copy(wv2.at[:, at], wring.at[slot, :, pl.ds(PAIR, PAIR)], wsem.at[slot]).start()
+
     def start_wo2(b, slot):
         for i in range(2):
             pltpu.make_async_copy(
@@ -134,7 +142,8 @@
         (base_up, base_up + part, start_mlp, None),
         (base_up + part, base_down, lambda r, slot: start_mlp(shared_tile(r), slot), None),
         (base_down, base_down + blocks, lambda r, slot: start_down(r, 0, slot), None),
-        (base_down + blocks, base2, lambda r, slot: start_down(r // 2, 1 + r % 2 if isinstance(r, int) else 1 + lax.rem(r, 2), slot), None),
+        (base_down + blocks, base_x, lambda r, slot: start_down(r // 2, 1 + r % 2 if isinstance(r, int) else 1 + lax.rem(r, 2), slot), None),
+        (base_x, base2, start_kv_other, None),
         (base2, base2 + qkv2, start_v2, 0),
         (base2, base2 + qkv2, start_qk2, 1),
         (base2, base2 + qkv2, start_qk2, 2),
@@ -498,7 +507,7 @@
             s = base_down + blocks + 2 * b + k
             slot = wait_tile(s, ffc)
             down = down + down_dot(slot, 1 + k)
-            start_tile(s + SLOTS, base_down + blocks + k + SLOTS, base2 - 1 + k + SLOTS)
+            start_tile(s + SLOTS, base_down + blocks + k + SLOTS, base_x - 1 + k + SLOTS)
         gbuf[pl.ds(chip_rows, crows), at] = (hbuf[:, at].astype(F32) + down).astype(BF16)
         piece = g_piece(b, chip_rows)
         remote(piece, piece, gxs.at[b], gxr.at[b], peer).start()
@@ -519,12 +528,31 @@
         c.start()
     norm(gbuf, nbuf, chip_rows, crows)
 
-    @pl.loop(0, blocks)
-    def _(b):
+    def g_forward(b):
         far = g_piece(b, far_rows)
         remote(far, far, gxs.at[b], gxr.at[b], peer).wait_recv()
         remote(far, far, dsend.at[0], drecv.at[0], partner).start()
 
+    @pl.loop(0, blocks - 1)
+    def _(b):
+        g_forward(b)
+
+    @pl.loop(0, blocks)
+    def _(b):
+        s = base_x + b
+        slot = wait_tile(s)
+        raw = jnp.dot(nbuf[pl.ds(chip_rows, crows), :], wring[slot], preferred_element_type=F32)
+        start_tile(s + SLOTS, base_x + SLOTS, base2 + SLOTS)
+        k_at = pl.ds(pl.multiple_of(b * TILE, 128), PAIR)
+        v_at = pl.ds(pl.multiple_of(b * TILE + PAIR, 128), PAIR)
+        ebuf[:, k_at] = biased_rope(raw[:, :PAIR], 3, other2 // HEAD + 2 * b, pl.ds(chip_rows, crows), 2)
+        ebuf[:, v_at] = raw[:, PAIR:].astype(BF16)
+        to_at = pl.ds(pl.multiple_of(other2 + b * PAIR, 128), PAIR)
+        for kv, (at, dst) in enumerate(((k_at, k2_out), (v_at, v2_out))):
+            pltpu.make_async_copy(ebuf.at[pl.ds(my_rows, rows), at], dst.at[:, to_at], a2send.at[2 * kv]).start()
+            remote(ebuf.at[pl.ds(other_rows, rows), at], dst.at[:, to_at], a2send.at[2 * kv + 1], a2recv.at[kv], partner).start()
+
+    g_forward(blocks - 1)
     g_wait(far_rows, 0)
     norm(gbuf, nbuf, far_rows, crows)
 
@@ -568,20 +596,14 @@
     def o2_copy(b):
         return remote(o2_far(b), o2_piece(b, chip), osend.at[b], orecv.at[b], peer)
 
-    def append2(b, kind):
-        who, to_core, to_chip = ((None, core, chip), (partner, 1 - core, chip), (peer, core, 1 - chip),
-                                 (diag, 1 - core, 1 - chip))[kind]
-        row_at = pl.ds(pl.multiple_of(to_chip * crows + to_core * rows, 16), rows)
+    def append2(b):
         to_at = pl.ds(pl.multiple_of(own2 + b * PAIR, 128), PAIR)
         v_at = pl.ds(pl.multiple_of(lax.rem(b, 2) * PAIR, 128), PAIR)
-        for kv, (part, dst) in enumerate(((pre.at[qk_tile(b), row_at, pl.ds(PAIR, PAIR)], k2_out),
-                                          (pre.at[3 * (b // 2), row_at, v_at], v2_out))):
-            if kind == 0:
-                pltpu.make_async_copy(part, dst.at[:, to_at], a2send.at[4 * kv]).start()
-            else:
-                remote(part, dst.at[:, to_at], a2send.at[4 * kv + kind], a2recv.at[4 * kv + kind], who).start()
-
-    early = 1
+        mine = pl.ds(pl.multiple_of(chip_rows + my_rows, 16), rows)
+        others = pl.ds(pl.multiple_of(chip_rows + other_rows, 16), rows)
+        for kv, (t, at, dst) in enumerate(((qk_tile(b), pl.ds(PAIR, PAIR), k2_out), (3 * (b // 2), v_at, v2_out))):
+            pltpu.make_async_copy(pre.at[t, mine, at], dst.at[:, to_at], a2send.at[2 * kv]).start()
+            remote(pre.at[t, others, at], dst.at[:, to_at], a2send.at[2 * kv + 1], a2recv.at[kv], partner).start()
 
     @pl.loop(0, qkv2)
     def _(t):
@@ -624,18 +646,7 @@
             obuf[:, pl.ds(pl.multiple_of(chip * quart + b * PAIR, 128), PAIR)] = opair[pl.ds(chip_rows, crows), :]
             obuf[:, pl.ds(pl.multiple_of(half + b * PAIR, 128), PAIR)] = opair[pl.ds(far_rows, crows), :]
             o2_copy(b).start()
-            append2(b, 0)
-            append2(b, 1)
-
-            @pl.when(b < early)
-            def _():
-                append2(b, 2)
-                append2(b, 3)
-
-    @pl.loop(early, blocks)
-    def _(b):
-        append2(b, 2)
-        append2(b, 3)
+            append2(b)
 
     @pl.loop(0, blocks)
     def _(b):
@@ -675,11 +686,10 @@
         remote(g_piece(b, chip_rows), g_piece(b, chip_rows), gxs.at[b], gxr.at[b], peer).wait_send()
 
     for kv, dst in enumerate((k2_out, v2_out)):
-        ref = dst.at[:, pl.ds(0, quart)]
-        pltpu.make_async_copy(ref, ref, a2send.at[4 * kv]).wait()
-        for kind, who in ((1, partner), (2, peer), (3, diag)):
-            remote(ref, ref, a2send.at[4 * kv + kind], a2recv.at[4 * kv + kind], who).wait_send()
-            remote(ref, ref, a2send.at[4 * kv + kind], a2recv.at[4 * kv + kind], who).wait_recv()
+        ref = dst.at[:, pl.ds(0, half)]
+        pltpu.make_async_copy(ref, ref, a2send.at[2 * kv]).wait()
+        remote(ref, ref, a2send.at[2 * kv + 1], a2recv.at[kv], partner).wait_send()
+        remote(ref, ref, a2send.at[2 * kv + 1], a2recv.at[kv], partner).wait_recv()
         for kind in (2, 3):
             cache2_copy(kv, kind).wait_send()
     for ref, sem in ((y_out, 1), (g_out, 0)):
@@ -738,7 +748,7 @@
                 dma((SLOTS,)), dma((3,)), dma((6,)), dma((8,)), dma((8, 6)),
                 dma((blocks,)), dma((blocks,)), dma((blocks,)), dma((blocks,)), dma((blocks,)), dma((blocks,)),
                 dma((5,)), dma((5,)), dma((6,)), dma((2,)),
-                dma((blocks,)), dma((blocks,)), dma((8,)), dma((8,)),
+                dma((blocks,)), dma((blocks,)), dma((4,)), dma((2,)),
                 dma((blocks,)), dma((blocks,)), dma((2,)), pltpu.SemaphoreType.REGULAR,
             ],
             compiler_params=pltpu.CompilerParams(

time: 176 us -> 168 us (0.955)
  Pallas kernels: 157 us -> 150 us
    pallas_call x1, Pallas kernels: 157 us -> 150 us  [forward(): pl.pallas_call(functools.partial(body, (d_model, ff, rows, cache_rows)),...]
where the time goes in v5:
time: 168 us
  Pallas kernels  150 us (89%)
  local copies, waits for them, and re-layouts  17.7 us (11%)
    pallas_call x1, Pallas kernels, forward(): pl.pallas_call(functools.partial(body, (d_model, ff, rows, cache_rows)),...  150 us
    reshape x2, local copies, waits for them, and re-layouts, flat(): return c.reshape(cache_rows, d_model)  9.71 us
    reshape x2, local copies, waits for them, and re-layouts, unblock(): return a.transpose(1, 0, 2).reshape(rows, d_model)  4.18 us
    unnamed x16, local copies, waits for them, and re-layouts  3.8 us

profile of v5, /device:TPU:0, one launch (start us, length us, event | category | flops | bytes accessed | tf_op | source)
XLA Modules:
  0.0 168.2 jit_solution(4731483831820987017)
XLA Ops:
  0.6 0.0 copy-start
  0.6 0.0 copy-start.1
  0.7 6.2 %copy_bitcast_fusion.2 = (bf16[256,5120]{1,0:T(8,128)(2,1)}, bf16[256,5120]{1,0:T(8,128)(2,1)}) fusion(bf16[32,8,40,128]{3,2,1,0:T(8,128)(2,1)} %bitcast.30, bf16[32,8,40,128]{3,2,1,0:T(8,128)(2,1)} %bitcast.31), kind=kLoop, calls=%fused_computation.2 | loop fusion | bytes 10485760 | tf_op jit(solution)/shard_map/reshape | solution.py:719
  6.8 0.0 copy-done
  6.8 0.0 copy-done.1
  6.8 3.5 %copy_bitcast_fusion = (bf16[256,5120]{1,0:T(8,128)(2,1)}, bf16[256,5120]{1,0:T(8,128)(2,1)}) fusion(bf16[32,8,40,128]{3,2,1,0:T(8,128)(2,1)S(1)} %bitcast.32, bf16[32,8,40,128]{3,2,1,0:T(8,128)(2,1)S(1)} %bitcast.33), kind=kLoop, calls=%fused_computation | loop fusion | bytes 10485760 | tf_op jit(solution)/shard_map/reshape | solution.py:719
  10.4 149.9 %shard_map.253 = (bf16[10,64,512]{2,1,0:T(8,128)(2,1)}, bf16[10,64,512]{2,1,0:T(8,128)(2,1)}, bf16[64,5120]{1,0:T(8,128)(2,1)}, bf16[64,5120]{1,0:T(8,128)(2,1)}...) custom-call(f32[256,128]{1,0:T(8,128)} %constant.4.clone.cos_ref, f32[256,128]{1,0:T(8,128)} %constant.5.clone.sin_ref, ...), custom_call_target="tpu_custom_call" | custom-call | tf_op jit(solution)/shard_map/pallas_call | solution.py:726
  160.2 0.0 copy-start.5
  160.3 0.0 copy-start.4
  160.3 0.0 copy-start.3
  160.3 2.1 %copy.30 = bf16[10,8,8,512]{3,2,0,1:T(8,128)(2,1)} copy(bf16[10,8,8,512]{3,2,1,0:T(8,128)(2,1)} %bitcast.45) | data formatting | bytes 1310720 | tf_op jit(solution)/shard_map/reshape | solution.py:764
  162.4 0.0 copy-start.2
  162.4 2.1 %copy.31 = bf16[10,8,8,512]{3,2,0,1:T(8,128)(2,1)} copy(bf16[10,8,8,512]{3,2,1,0:T(8,128)(2,1)} %bitcast.44) | data formatting | bytes 1310720 | tf_op jit(solution)/shard_map/reshape | solution.py:764
  164.5 0.0 copy-done.5
  164.5 0.9 copy.36
  165.4 0.0 copy-done.4
  165.4 0.9 copy.37
  166.4 0.0 copy-done.3
  166.4 0.9 copy.38
  167.3 0.0 copy-done.2
  167.3 0.9 copy.39
Async XLA Ops:
  0.6 6.2 %copy-start = (bf16[256,40,128]{2,1,0:T(8,128)(2,1)S(1)}, bf16[256,40,128]{2,1,0:T(8,128)(2,1)}, u32[]{:S(2)}) copy-start(bf16[256,40,128]{2,1,0:T(8,128)(2,1)} %param.35) | copy-start | bytes 7864324
  0.6 6.2 %copy-start.1 = (bf16[256,40,128]{2,1,0:T(8,128)(2,1)S(1)}, bf16[256,40,128]{2,1,0:T(8,128)(2,1)}, u32[]{:S(2)}) copy-start(bf16[256,40,128]{2,1,0:T(8,128)(2,1)} %param.34) | copy-start | bytes 7864324
  160.2 4.2 %copy-start.5 = (bf16[64,5120]{1,0:T(8,128)(2,1)S(1)}, bf16[64,5120]{1,0:T(8,128)(2,1)}, u32[]{:S(2)}) copy-start(bf16[64,5120]{1,0:T(8,128)(2,1)} %get-tuple-element.14) | copy-start | bytes 1966084
  160.3 5.1 %copy-start.4 = (bf16[64,5120]{1,0:T(8,128)(2,1)S(1)}, bf16[64,5120]{1,0:T(8,128)(2,1)}, u32[]{:S(2)}) copy-start(bf16[64,5120]{1,0:T(8,128)(2,1)} %get-tuple-element.15) | copy-start | bytes 1966084
  160.3 6.1 %copy-start.3 = (bf16[64,5120]{1,0:T(8,128)(2,1)S(1)}, bf16[64,5120]{1,0:T(8,128)(2,1)}, u32[]{:S(2)}) copy-start(bf16[64,5120]{1,0:T(8,128)(2,1)} %get-tuple-element.16) | copy-start | bytes 1966084
  162.4 4.9 %copy-start.2 = (bf16[64,5120]{1,0:T(8,128)(2,1)S(1)}, bf16[64,5120]{1,0:T(8,128)(2,1)}, u32[]{:S(2)}) copy-start(bf16[64,5120]{1,0:T(8,128)(2,1)} %get-tuple-element.17) | copy-start | bytes 1966084

commit v6 on v5

--- a/solution.py
+++ b/solution.py
@@ -29,12 +29,12 @@
     return np.concatenate([cos_t, cos_t], axis=1), np.concatenate([-sin_t, sin_t], axis=1)
 
 
-def body(dims, cos_ref, sin_ref, bq1, bk1, bq2, bk2, x_hbm, ck1, cv1, ck2, cv2, wq1, wk1, wv1, wo1, w_gate, w_up, w_down,
-         wq2, wk2, wv2, wo2, g_out, y_out, k1_out, v1_out, k2_out, v2_out,
+def body(dims, cos_ref, sin_ref, bq1, bk1, bq2, bk2, x_hbm, raw_k1, raw_v1, raw_k2, raw_v2, wq1, wk1, wv1, wo1, w_gate, w_up, w_down,
+         wq2, wk2, wv2, wo2, g_out, y_out, k1_out, v1_out, k2_out, v2_out, ck1, cv1, ck2, cv2,
          wring, nbuf, gbuf, ebuf, pre, kc, vc, o_loc, o_send, o_recv, obuf, opair,
          st_loc, st_send, st_recv, bias32,
          wsem, xsem, csem, c2send, c2recv, qsend, qrecv, osend, orecv, ssend, srecv, dsend, drecv, asem, gsem,
-         gxs, gxr, a2send, a2recv, hys, hyr, esem, yfree):
+         gxs, gxr, a2send, a2recv, hys, hyr, esem, yfree, rawbuf, psem, fsem):
     d_model, ff, rows, cache_rows = dims
     half = d_model // 2
     ffh = ff // 2
@@ -181,6 +181,29 @@
         return pltpu.make_async_remote_copy(src_ref=src, dst_ref=dst, send_sem=send, recv_sem=recv,
                                             device_id={"dp": side_y}, device_id_type=MESH)
 
+    HEADS8 = 8
+    WIDE = HEADS8 * HEAD
+    groups = d_model // WIDE
+
+    def raw_copy(raw, j, slot):
+        return pltpu.make_async_copy(raw.at[:, pl.ds(pl.multiple_of(j * HEADS8, HEADS8), HEADS8), :], rawbuf.at[slot],
+                                     psem.at[slot])
+
+    def flat_wait(flat, slot):
+        ref = flat.at[:, pl.ds(0, WIDE)]
+        pltpu.make_async_copy(ref, ref, fsem.at[slot]).wait()
+
+    def flatten_heads(flat, j, slot):
+        for i in range(cache_rows // crows):
+            at = pl.ds((slot * 2 + i) * WIDE, WIDE)
+            ebuf[:, at] = pltpu.einshape("thd->t(hd)", rawbuf[slot, i * crows:(i + 1) * crows])
+            pltpu.make_async_copy(ebuf.at[:, at], flat.at[pl.ds(i * crows, crows), pl.ds(pl.multiple_of(j * WIDE, 128), WIDE)],
+                                  fsem.at[slot]).start()
+
+    layer1 = ((raw_k1, ck1), (raw_v1, cv1))
+    layer2 = ((raw_k2, ck2), (raw_v2, cv2))
+    for slot in range(2):
+        raw_copy(layer1[slot][0], 0, slot).start()
     for s in range(2):
         start_tile(s, s, s + 1)
 
@@ -204,6 +227,24 @@
                               partner))
         return out
 
+    @pl.loop(0, groups)
+    def _(j):
+        for slot, (raw, flat) in enumerate(layer1):
+            raw_copy(raw, j, slot).wait()
+
+            @pl.when(j > 0)
+            def _():
+                flat_wait(flat, slot)
+
+            flatten_heads(flat, j, slot)
+
+            @pl.when(j < groups - 1)
+            def _():
+                raw_copy(raw, j + 1, slot).start()
+
+    for slot, (raw, flat) in enumerate(layer1):
+        flat_wait(flat, slot)
+        raw_copy(layer2[slot][0], 0, slot).start()
     cache1 = cache_copies(ck1, cv1)
     for c in cache1:
         c.start()
@@ -317,6 +358,21 @@
                        asem.at[k + 2], partner).start()
             o_copy(b).start()
             s_copy(b).start()
+            for slot, (raw, flat) in enumerate(layer2):
+                raw_copy(raw, b, slot).wait()
+
+                @pl.when(b > 0)
+                def _():
+                    flat_wait(flat, slot)
+
+                flatten_heads(flat, b, slot)
+
+                @pl.when(b < blocks - 1)
+                def _():
+                    raw_copy(raw, b + 1, slot).start()
+
+        for slot, (raw, flat) in enumerate(layer2):
+            flat_wait(flat, slot)
 
         @pl.loop(0, blocks)
         def _(b):
@@ -523,7 +579,7 @@
     far_cache(4)
     g_wait(chip_rows, 3)
     g_rows = pl.ds(pl.multiple_of(chip_rows + my_rows, 16), rows)
-    g_copies = [pltpu.make_async_copy(gbuf.at[g_rows, pl.ds(j * TILE, TILE)], g_out.at[j], gsem.at[0]) for j in range(2 * blocks)]
+    g_copies = [pltpu.make_async_copy(gbuf.at[g_rows, :], g_out, gsem.at[0])]
     for c in g_copies:
         c.start()
     norm(gbuf, nbuf, chip_rows, crows)
@@ -675,7 +731,7 @@
             at = pl.ds(i * rows, rows)
             ybuf[:, pl.ds(pl.multiple_of(b * 2 * TILE + i * TILE, 128), TILE)] = (o_loc[b, at, :] + o_recv[b, at, :]).astype(BF16)
 
-    y_copies = [pltpu.make_async_copy(ybuf.at[:, pl.ds(j * TILE, TILE)], y_out.at[j], gsem.at[1]) for j in range(2 * blocks)]
+    y_copies = [pltpu.make_async_copy(ybuf, y_out, gsem.at[1])]
     for c in y_copies:
         c.start()
 
@@ -696,6 +752,12 @@
         pltpu.make_async_copy(ref, ref, gsem.at[sem]).wait()
 
 
+def deliver(*refs):
+    for i in range(6):
+        src, dst = refs[i], refs[6 + i]
+        dst[...] = src[...] if i < 2 else pltpu.einshape("t(hd)->thd", src[...], d=HEAD)
+
+
 def solution(mesh):
     rows_spec = P(('dp', 'cp'), None)
     cache_spec = P(('dp', 'cp'), None, None)
@@ -715,19 +777,15 @@
         cos_t, sin_t = rope_tables(4 * cache_rows + np.arange(2 * crows), head_dim)
         bias = [v.reshape(heads, head_dim) for v in (b_q1, b_k1, b_q2, b_k2)]
 
-        def flat(c):
-            return c.reshape(cache_rows, d_model)
-
         any_spec = pl.BlockSpec(memory_space=pl.ANY)
         vmem_spec = pl.BlockSpec(memory_space=pltpu.VMEM)
-        blocked = jax.ShapeDtypeStruct((2 * blocks, rows, TILE), BF16)
         row_out = jax.ShapeDtypeStruct((rows, d_model), BF16)
         dma = pltpu.SemaphoreType.DMA
         out = pl.pallas_call(
             functools.partial(body, (d_model, ff, rows, cache_rows)),
-            out_shape=[blocked] * 2 + [row_out] * 4,
+            out_shape=[row_out] * 6 + [jax.ShapeDtypeStruct((cache_rows, d_model), BF16)] * 4,
             in_specs=[vmem_spec] * 6 + [any_spec] * 16,
-            out_specs=[any_spec] * 6,
+            out_specs=[any_spec] * 10,
             scratch_shapes=[
                 pltpu.VMEM((SLOTS, d_model, TILE), BF16),
                 pltpu.VMEM((2 * crows, d_model), BF16),
@@ -750,19 +808,22 @@
                 dma((5,)), dma((5,)), dma((6,)), dma((2,)),
                 dma((blocks,)), dma((blocks,)), dma((4,)), dma((2,)),
                 dma((blocks,)), dma((blocks,)), dma((2,)), pltpu.SemaphoreType.REGULAR,
+                pltpu.VMEM((2, cache_rows, 8, head_dim), BF16), dma((2,)), dma((2,)),
             ],
             compiler_params=pltpu.CompilerParams(
                 collective_id=0, has_side_effects=True, vmem_limit_bytes=67043328),
-        )(cos_t, sin_t, *bias, x_in, flat(cache_k1), flat(cache_v1), flat(cache_k2), flat(cache_v2),
+        )(cos_t, sin_t, *bias, x_in, cache_k1, cache_v1, cache_k2, cache_v2,
           w_q1, w_k1, w_v1, w_o1, w_gate, w_up, w_down, w_q2, w_k2, w_v2, w_o2)
-        g, y2, k1, v1, k2, v2 = out
-
-        def heads_of(a):
-            return a.reshape(rows, heads, head_dim)
-
-        def unblock(a):
-            return a.transpose(1, 0, 2).reshape(rows, d_model)
-
-        return unblock(g), unblock(y2), heads_of(k1), heads_of(v1), heads_of(k2), heads_of(v2)
+        steps = 4
+        step_rows = pl.BlockSpec((rows // steps, d_model), lambda i: (i, 0))
+        step_heads = pl.BlockSpec((rows // steps, heads, head_dim), lambda i: (i, 0, 0))
+        head_out = jax.ShapeDtypeStruct((rows, heads, head_dim), BF16)
+        return pl.pallas_call(
+            deliver,
+            grid=(steps,),
+            out_shape=[row_out] * 2 + [head_out] * 4,
+            in_specs=[step_rows] * 6,
+            out_specs=[step_rows] * 2 + [step_heads] * 4,
+        )(*out[:6])
 
     return jax.shard_map(forward, mesh=mesh, in_specs=in_specs, out_specs=out_specs, check_vma=False)

time: 168 us -> 163 us (0.970)
  local copies, waits for them, and re-layouts: 17.7 us -> 0 us
  Pallas kernels: 150 us -> 162 us
    reshape x4 -> x0, local copies, waits for them, and re-layouts: 13.9 us -> none  [the longest x2 9.71 us: flat(): return c.reshape(cache_rows, d_model)]
    pallas_call x1, Pallas kernels: 150 us -> 157 us  [forward(): pl.pallas_call(functools.partial(body, (d_model, ff, rows, cache_rows)),...]
    pallas_call x0 -> x1, Pallas kernels: none -> 4.6 us  [forward(): pl.pallas_call(deliver, grid=(steps,), out_shape=[row_out] * 2 + [head_ou...]
    unnamed x16 -> x0, local copies, waits for them, and re-layouts: 3.8 us -> none
where the time goes in v6:
time: 163 us
  Pallas kernels  162 us (99%)
    pallas_call x1, Pallas kernels, forward(): pl.pallas_call(functools.partial(body, (d_model, ff, rows, cache_rows)),...  157 us
    pallas_call x1, Pallas kernels, forward(): pl.pallas_call(deliver, grid=(steps,), out_shape=[row_out] * 2 + [head_ou...  4.6 us

profile of v6, /device:TPU:0, one launch (start us, length us, event | category | flops | bytes accessed | tf_op | source)
XLA Modules:
  0.0 162.7 jit_solution(8195399002475788330)
XLA Ops:
  0.6 157.3 %shard_map.253 = (bf16[64,5120]{1,0:T(8,128)(2,1)}, bf16[64,5120]{1,0:T(8,128)(2,1)}, bf16[64,5120]{1,0:T(8,128)(2,1)}, bf16[64,5120]{1,0:T(8,128)(2,1)}, bf16[6...) custom-call(f32[256,128]{1,0:T(8,128)} %constant.4.clone.cos_ref, ...), custom_call_target="tpu_custom_call" | custom-call | tf_op jit(solution)/shard_map/pallas_call | solution.py:784
  157.9 4.6 %shard_map.254 = (bf16[64,5120]{1,0:T(8,128)(2,1)}, bf16[64,5120]{1,0:T(8,128)(2,1)}, bf16[64,40,128]{2,1,0:T(8,128)(2,1)}, bf16[64,40,128]{2,1,0:T(8,128)(2,1)}...) custom-call(bf16[64,5120]{1,0:T(8,128)(2,1)} %get-tuple-element.12.refs_0_, ...), custom_call_target="tpu_custom_call" | custom-call | tf_op jit(solution)/shard_map/pallas_call | solution.py:821

commit v7 on v6

--- a/solution.py
+++ b/solution.py
@@ -30,7 +30,7 @@
 
 
 def body(dims, cos_ref, sin_ref, bq1, bk1, bq2, bk2, x_hbm, raw_k1, raw_v1, raw_k2, raw_v2, wq1, wk1, wv1, wo1, w_gate, w_up, w_down,
-         wq2, wk2, wv2, wo2, g_out, y_out, k1_out, v1_out, k2_out, v2_out, ck1, cv1, ck2, cv2,
+         wq2, wk2, wv2, wo2, g_out, y_out, k1_out, v1_out, k2_out, v2_out, ck2, cv2,
          wring, nbuf, gbuf, ebuf, pre, kc, vc, o_loc, o_send, o_recv, obuf, opair,
          st_loc, st_send, st_recv, bias32,
          wsem, xsem, csem, c2send, c2recv, qsend, qrecv, osend, orecv, ssend, srecv, dsend, drecv, asem, gsem,
@@ -200,11 +200,12 @@
             pltpu.make_async_copy(ebuf.at[:, at], flat.at[pl.ds(i * crows, crows), pl.ds(pl.multiple_of(j * WIDE, 128), WIDE)],
                                   fsem.at[slot]).start()
 
-    layer1 = ((raw_k1, ck1), (raw_v1, cv1))
+    layer1 = ((raw_k1, kc), (raw_v1, vc))
     layer2 = ((raw_k2, ck2), (raw_v2, cv2))
-    for slot in range(2):
-        raw_copy(layer1[slot][0], 0, slot).start()
-    for s in range(2):
+    for j in range(2):
+        for kv in range(2):
+            raw_copy(layer1[kv][0], j, 2 * j + kv).start()
+    for s in range(3):
         start_tile(s, s, s + 1)
 
     barrier = pltpu.get_barrier_semaphore()
@@ -218,37 +219,41 @@
     x_rem.start()
     x_loc.start()
 
-    def cache_copies(ck, cv):
-        crow = pl.ds(pl.multiple_of(core * cache_rows, 16), cache_rows)
-        out = []
-        for i, (src, dst) in enumerate(((ck, kc), (cv, vc))):
-            out.append(pltpu.make_async_copy(src.at[:, pl.ds(my_cols, half)], dst.at[crow], csem.at[3 * i]))
-            out.append(remote(src.at[:, pl.ds(other_cols, half)], dst.at[crow], csem.at[3 * i + 1], csem.at[3 * i + 2],
-                              partner))
-        return out
+    crow = pl.ds(pl.multiple_of(core * cache_rows, 16), cache_rows)
+    cache1 = [remote(c.at[crow], c.at[crow], csem.at[2 * kv], csem.at[2 * kv + 1], partner) for kv, c in enumerate((kc, vc))]
 
     @pl.loop(0, groups)
     def _(j):
-        for slot, (raw, flat) in enumerate(layer1):
+        for kv, (raw, cache) in enumerate(layer1):
+            slot = 2 * lax.rem(j, 2) + kv
             raw_copy(raw, j, slot).wait()
-
-            @pl.when(j > 0)
+            for i in range(cache_rows // crows):
+                rows_at = pl.ds(pl.multiple_of(core * cache_rows + i * crows, 16), crows)
+                vals = pltpu.einshape("thd->t(hd)", rawbuf[slot, i * crows:(i + 1) * crows])
+                for part_i in range(WIDE // TILE):
+                    piece = vals[:, part_i * TILE:(part_i + 1) * TILE]
+                    block = 2 * j + part_i
+                    owner = block // blocks
+                    block = block - owner * blocks
+                    to_at = pl.ds(pl.multiple_of(block * TILE, 128), TILE)
+
+                    @pl.when(owner == core)
+                    def _():
+                        cache[rows_at, to_at] = piece
+
+                    @pl.when(owner != core)
+                    def _():
+                        at = pl.ds(pl.multiple_of(((block * 2 + kv) * 2 + i) * TILE, 128), TILE)
+                        ebuf[:, at] = piece
+                        remote(ebuf.at[:, at], cache.at[rows_at, to_at], csem.at[2 * kv], csem.at[2 * kv + 1], partner).start()
+
+            @pl.when(j < groups - 2)
             def _():
-                flat_wait(flat, slot)
-
-            flatten_heads(flat, j, slot)
-
-            @pl.when(j < groups - 1)
-            def _():
-                raw_copy(raw, j + 1, slot).start()
-
-    for slot, (raw, flat) in enumerate(layer1):
-        flat_wait(flat, slot)
-        raw_copy(layer2[slot][0], 0, slot).start()
-    cache1 = cache_copies(ck1, cv1)
-    for c in cache1:
-        c.start()
-    for s in range(2, SLOTS):
+                raw_copy(raw, j + 2, slot).start()
+
+    for slot, (raw, flat) in enumerate(layer2):
+        raw_copy(raw, 0, slot).start()
+    for s in range(3, SLOTS):
         start_tile(s, s, s + 1)
     for i, ref in enumerate((bq1, bk1, bq2, bk2)):
         bias32[i] = ref[...].astype(F32)
@@ -783,9 +788,9 @@
         dma = pltpu.SemaphoreType.DMA
         out = pl.pallas_call(
             functools.partial(body, (d_model, ff, rows, cache_rows)),
-            out_shape=[row_out] * 6 + [jax.ShapeDtypeStruct((cache_rows, d_model), BF16)] * 4,
+            out_shape=[row_out] * 6 + [jax.ShapeDtypeStruct((cache_rows, d_model), BF16)] * 2,
             in_specs=[vmem_spec] * 6 + [any_spec] * 16,
-            out_specs=[any_spec] * 10,
+            out_specs=[any_spec] * 8,
             scratch_shapes=[
                 pltpu.VMEM((SLOTS, d_model, TILE), BF16),
                 pltpu.VMEM((2 * crows, d_model), BF16),
@@ -803,12 +808,12 @@
                 pltpu.VMEM((blocks, 8, HEAD), F32),
                 pltpu.VMEM((blocks, 8, HEAD), F32),
                 pltpu.VMEM((4, heads, head_dim), F32),
-                dma((SLOTS,)), dma((3,)), dma((6,)), dma((8,)), dma((8, 6)),
+                dma((SLOTS,)), dma((3,)), dma((4,)), dma((8,)), dma((8, 6)),
                 dma((blocks,)), dma((blocks,)), dma((blocks,)), dma((blocks,)), dma((blocks,)), dma((blocks,)),
                 dma((5,)), dma((5,)), dma((6,)), dma((2,)),
                 dma((blocks,)), dma((blocks,)), dma((4,)), dma((2,)),
                 dma((blocks,)), dma((blocks,)), dma((2,)), pltpu.SemaphoreType.REGULAR,
-                pltpu.VMEM((2, cache_rows, 8, head_dim), BF16), dma((2,)), dma((2,)),
+                pltpu.VMEM((4, cache_rows, 8, head_dim), BF16), dma((4,)), dma((2,)),
             ],
             compiler_params=pltpu.CompilerParams(
                 collective_id=0, has_side_effects=True, vmem_limit_bytes=67043328),

time: 163 us -> 160 us (0.982)
  Pallas kernels: 162 us -> 159 us
    pallas_call x1, Pallas kernels: 157 us -> 154 us  [forward(): pl.pallas_call(functools.partial(body, (d_model, ff, rows, cache_rows)),...]
where the time goes in v7:
time: 160 us; the launch traced here: 159 us
  Pallas kernels  159 us (99%)
    pallas_call x1, Pallas kernels, forward(): pl.pallas_call(functools.partial(body, (d_model, ff, rows, cache_rows)),...  154 us
    pallas_call x1, Pallas kernels, forward(): pl.pallas_call(deliver, grid=(steps,), out_shape=[row_out] * 2 + [head_ou...  4.6 us

profile of v7, /device:TPU:0, one launch (start us, length us, event | category | flops | bytes accessed | tf_op | source)
XLA Modules:
  0.0 159.5 jit_solution(3647359302055106230)
XLA Ops:
  0.6 154.1 %shard_map.253 = (bf16[64,5120]{1,0:T(8,128)(2,1)}, bf16[64,5120]{1,0:T(8,128)(2,1)}, bf16[64,5120]{1,0:T(8,128)(2,1)}, bf16[64,5120]{1,0:T(8,128)(2,1)}, bf16[6...) custom-call(f32[256,128]{1,0:T(8,128)} %constant.4.clone.cos_ref, ...), custom_call_target="tpu_custom_call" | custom-call | tf_op jit(solution)/shard_map/pallas_call | solution.py:789
  154.7 4.6 %shard_map.254 = (bf16[64,5120]{1,0:T(8,128)(2,1)}, bf16[64,5120]{1,0:T(8,128)(2,1)}, bf16[64,40,128]{2,1,0:T(8,128)(2,1)}, bf16[64,40,128]{2,1,0:T(8,128)(2,1)}...) custom-call(bf16[64,5120]{1,0:T(8,128)(2,1)} %get-tuple-element.12.refs_0_, ...), custom_call_target="tpu_custom_call" | custom-call | tf_op jit(solution)/shard_map/pallas_call | solution.py:826

commit v8 on v7

--- a/solution.py
+++ b/solution.py
@@ -222,39 +222,43 @@
     crow = pl.ds(pl.multiple_of(core * cache_rows, 16), cache_rows)
     cache1 = [remote(c.at[crow], c.at[crow], csem.at[2 * kv], csem.at[2 * kv + 1], partner) for kv, c in enumerate((kc, vc))]
 
-    @pl.loop(0, groups)
-    def _(j):
-        for kv, (raw, cache) in enumerate(layer1):
-            slot = 2 * lax.rem(j, 2) + kv
-            raw_copy(raw, j, slot).wait()
-            for i in range(cache_rows // crows):
-                rows_at = pl.ds(pl.multiple_of(core * cache_rows + i * crows, 16), crows)
-                vals = pltpu.einshape("thd->t(hd)", rawbuf[slot, i * crows:(i + 1) * crows])
-                for part_i in range(WIDE // TILE):
-                    piece = vals[:, part_i * TILE:(part_i + 1) * TILE]
-                    block = 2 * j + part_i
-                    owner = block // blocks
-                    block = block - owner * blocks
-                    to_at = pl.ds(pl.multiple_of(block * TILE, 128), TILE)
-
-                    @pl.when(owner == core)
-                    def _():
-                        cache[rows_at, to_at] = piece
-
-                    @pl.when(owner != core)
-                    def _():
-                        at = pl.ds(pl.multiple_of(((block * 2 + kv) * 2 + i) * TILE, 128), TILE)
-                        ebuf[:, at] = piece
-                        remote(ebuf.at[:, at], cache.at[rows_at, to_at], csem.at[2 * kv], csem.at[2 * kv + 1], partner).start()
-
-            @pl.when(j < groups - 2)
-            def _():
-                raw_copy(raw, j + 2, slot).start()
-
-    for slot, (raw, flat) in enumerate(layer2):
-        raw_copy(raw, 0, slot).start()
-    for s in range(3, SLOTS):
-        start_tile(s, s, s + 1)
+    def place_cache1():
+        start_tile(3, 3, 4)
+
+        @pl.loop(0, groups)
+        def _(j):
+            for kv, (raw, cache) in enumerate(layer1):
+                slot = 2 * lax.rem(j, 2) + kv
+                raw_copy(raw, j, slot).wait()
+                for i in range(cache_rows // crows):
+                    rows_at = pl.ds(pl.multiple_of(core * cache_rows + i * crows, 16), crows)
+                    vals = pltpu.einshape("thd->t(hd)", rawbuf[slot, i * crows:(i + 1) * crows])
+                    for part_i in range(WIDE // TILE):
+                        piece = vals[:, part_i * TILE:(part_i + 1) * TILE]
+                        block = 2 * j + part_i
+                        owner = block // blocks
+                        block = block - owner * blocks
+                        to_at = pl.ds(pl.multiple_of(block * TILE, 128), TILE)
+
+                        @pl.when(owner == core)
+                        def _():
+                            cache[rows_at, to_at] = piece
+
+                        @pl.when(owner != core)
+                        def _():
+                            at = pl.ds(pl.multiple_of(((block * 2 + kv) * 2 + i) * TILE, 128), TILE)
+                            ebuf[:, at] = piece
+                            remote(ebuf.at[:, at], cache.at[rows_at, to_at], csem.at[2 * kv], csem.at[2 * kv + 1], partner).start()
+
+                @pl.when(j < groups - 2)
+                def _():
+                    raw_copy(raw, j + 2, slot).start()
+
+        for slot, (raw, flat) in enumerate(layer2):
+            raw_copy(raw, 0, slot).start()
+        for s in range(4, SLOTS):
+            start_tile(s, s, s + 1)
+
     for i, ref in enumerate((bq1, bk1, bq2, bk2)):
         bias32[i] = ref[...].astype(F32)
     x_loc.wait()
@@ -317,6 +321,21 @@
     def s_copy(b):
         return remote(st_send.at[b], st_recv.at[b], ssend.at[b], srecv.at[b], peer)
 
+    PIECE = TILE // 2
+
+    def cache2_copy(kv, kind, b=None):
+        src, dst = ((ck2, kc), (cv2, vc))[kv]
+        who, to_core, to_chip = ((None, core, chip), (partner, 1 - core, chip), (peer, core, 1 - chip),
+                                 (diag, 1 - core, 1 - chip))[kind]
+        off, width, sem = (0, quart, 0) if b is None else (b * PIECE, PIECE, 1 + b)
+        side = 0 if kind < 2 else quart
+        from_at = pl.ds(pl.multiple_of(to_core * half + to_chip * quart + off, 128), width)
+        to = dst.at[pl.ds(pl.multiple_of(core * cache_rows, 16), cache_rows), pl.ds(pl.multiple_of(side + off, 128), width)]
+        i = 4 * kv + kind
+        if kind == 0:
+            return pltpu.make_async_copy(src.at[:, from_at], to, c2send.at[i])
+        return remote(src.at[:, from_at], to, c2send.at[i], c2recv.at[i, sem], who)
+
     def head_of(b):
         return core * (half // HEAD) + b * PER_BLOCK
 
@@ -329,6 +348,7 @@
             q_copy(b).start()
 
         q_step(0, base, base, base + 1)
+        place_cache1()
 
         @pl.loop(0, blocks)
         def _(b):
@@ -383,6 +403,13 @@
         def _(b):
             o_copy(b).wait_recv()
             s_copy(b).wait_recv()
+
+            @pl.when(b == blocks - 1)
+            def _():
+                for piece in range(3):
+                    for kv in range(2):
+                        cache2_copy(kv, 2, piece).start()
+
             far = jnp.concatenate([st_recv[b], jnp.zeros((HEAD - 8, HEAD), F32)], axis=0).T
             near = st_loc[b]
             for i in range(PER_BLOCK):
@@ -424,28 +451,14 @@
     attention(xin, base1, 0, cache1, k1_out, v1_out)
     pl.semaphore_signal(yfree, inc=1, device_id={"dp": side_y}, device_id_type=MESH)
 
-    PIECE = TILE // 2
-
-    def cache2_copy(kv, kind, b=None):
-        src, dst = ((ck2, kc), (cv2, vc))[kv]
-        who, to_core, to_chip = ((None, core, chip), (partner, 1 - core, chip), (peer, core, 1 - chip),
-                                 (diag, 1 - core, 1 - chip))[kind]
-        off, width, sem = (0, quart, 0) if b is None else (b * PIECE, PIECE, 1 + b)
-        side = 0 if kind < 2 else quart
-        from_at = pl.ds(pl.multiple_of(to_core * half + to_chip * quart + off, 128), width)
-        to = dst.at[pl.ds(pl.multiple_of(core * cache_rows, 16), cache_rows), pl.ds(pl.multiple_of(side + off, 128), width)]
-        i = 4 * kv + kind
-        if kind == 0:
-            return pltpu.make_async_copy(src.at[:, from_at], to, c2send.at[i])
-        return remote(src.at[:, from_at], to, c2send.at[i], c2recv.at[i, sem], who)
-
     def far_cache(b):
         for kv in range(2):
             for kind in (2, 3):
                 cache2_copy(kv, kind, b).start()
 
     for b in range(3):
-        far_cache(b)
+        for kv in range(2):
+            cache2_copy(kv, 3, b).start()
     for kind in (1, 0):
         for kv in range(2):
             cache2_copy(kv, kind).start()

time: 160 us -> 163 us (1.019)
  Pallas kernels: 159 us -> 162 us
    pallas_call x1, Pallas kernels: 154 us -> 157 us  [forward(): pl.pallas_call(functools.partial(body, (d_model, ff, rows, cache_rows)),...]
where the time goes in v8:
time: 163 us; the launch traced here: 162 us
  Pallas kernels  162 us (99%)
    pallas_call x1, Pallas kernels, forward(): pl.pallas_call(functools.partial(body, (d_model, ff, rows, cache_rows)),...  157 us
    pallas_call x1, Pallas kernels, forward(): pl.pallas_call(deliver, grid=(steps,), out_shape=[row_out] * 2 + [head_ou...  4.6 us

profile of v8, /device:TPU:0, one launch (start us, length us, event | category | flops | bytes accessed | tf_op | source)
XLA Modules:
  0.0 162.4 jit_solution(14567475676153554182)
XLA Ops:
  0.6 157.0 %shard_map.253 = (bf16[64,5120]{1,0:T(8,128)(2,1)}, bf16[64,5120]{1,0:T(8,128)(2,1)}, bf16[64,5120]{1,0:T(8,128)(2,1)}, bf16[64,5120]{1,0:T(8,128)(2,1)}, bf16[6...) custom-call(f32[256,128]{1,0:T(8,128)} %constant.4.clone.cos_ref, ...), custom_call_target="tpu_custom_call" | custom-call | tf_op jit(solution)/shard_map/pallas_call | solution.py:802
  157.6 4.6 %shard_map.254 = (bf16[64,5120]{1,0:T(8,128)(2,1)}, bf16[64,5120]{1,0:T(8,128)(2,1)}, bf16[64,40,128]{2,1,0:T(8,128)(2,1)}, bf16[64,40,128]{2,1,0:T(8,128)(2,1)}...) custom-call(bf16[64,5120]{1,0:T(8,128)(2,1)} %get-tuple-element.12.refs_0_, ...), custom_call_target="tpu_custom_call" | custom-call | tf_op jit(solution)/shard_map/pallas_call | solution.py:839
